TPU v7x, 256 devices: a whole 4x4x8 slice. The times are simulated.
256 devices in a mesh: seq: 64 (over z, y, core), feat: 4 (over x).
Axes of the slice: x: 4, y: 4, z: 8, core: 2. Of those that a mesh axis runs over, the one named last changes fastest.
Arguments:
- hidden_in: bfloat16 [4, 16384, 2048], P(None, 'seq'), may hold values from -6 to 6
- w_query: bfloat16 [2048, 256], replicated, may hold values from -0.125 to 0.125
- w_key: bfloat16 [2048, 256], replicated, may hold values from -0.125 to 0.125
- w_value: bfloat16 [2048, 2048], P(None, 'feat'), may hold values from -0.125 to 0.125
- lengths: int32 [4], replicated, may hold values from 8192 to 16384, as said below
- owners: int32 [4], replicated, may hold values from 0 to 63
Outputs:
- mixed: bfloat16 [4, 16384, 2048], P(None, 'seq', 'feat')
- state_quad: float32 [64, 4, 16, 256, 128], P('seq', None, None, 'feat')
- state_low: float32 [64, 4, 16, 17, 128], P('seq', None, 'feat')
- norm_quad: float32 [64, 4, 16, 256], P('seq', None, None, 'feat')
- norm_low: float32 [64, 4, 16, 17], P('seq', None, 'feat')
Inputs may be any that keep to these rules, and one draw needn't show every extreme that they name: `lengths`: every prompt holds 8192 to 16384 live tokens, and some prompt holds exactly 16384. `owners`: several prompts may share a decoding device.
All inputs are finite; a program needn't handle non-finite values.
Results may differ from a plain program's by a relative error of at most 0.0085.
Values may be sent and summed in bfloat16 or wider, within the bound.
A program may use at most 256 MiB of HBM per device.

v0:
```python
import jax
import jax.numpy as jnp
from jax import lax
from jax.sharding import Mesh
from jax.sharding import PartitionSpec as P

H = 16
FD = 16
SEQ = ("seq_0", "seq_1", "seq_2")


NORM_FLOOR = 0.0001


def nothing_yet(shard, identity):
    return jax.tree.map(
        lambda a, e: jnp.broadcast_to(jnp.asarray(e, a.dtype), a.shape), shard, identity
    )


def carried_in(shard, axes, combine, identity):
    before = start = nothing_yet(shard, identity)
    total = shard
    for axis in reversed(axes):
        peers, mine = (lax.axis_size(axis), lax.axis_index(axis))
        pieces = jax.tree.map(
            lambda part, kind: lax.all_gather(part.astype(kind), axis),
            total,
            (jnp.bfloat16, jnp.bfloat16, jnp.bfloat16, jnp.bfloat16),
        )
        inside, total = (start, start)
        for k in range(peers):
            passed = k < mine
            total = combine(
                total, jax.tree.map(lambda part, own: part[k].astype(own.dtype), pieces, shard)
            )
            inside = jax.tree.map(lambda new, old: jnp.where(passed, new, old), total, inside)
        before = combine(inside, before)
    return before


def in_one(arrays, axis):
    ends = [0]
    for a in arrays:
        ends.append(ends[-1] + a.size)
    total = lax.psum(jnp.concatenate([a.ravel() for a in arrays]), axis)
    return tuple((total[b:e].reshape(a.shape) for a, b, e in zip(arrays, ends, ends[1:])))


def low_features(inputs):
    constant = jnp.ones(inputs.shape[:-1] + (1,), jnp.float32)
    return jnp.concatenate([constant, inputs * FD ** (-0.25)], axis=-1)


def quad_features(leading, inputs):
    products = leading[..., :, None] * inputs[..., None, :]
    return products.reshape(inputs.shape[:-1] + (leading.shape[-1] * inputs.shape[-1],)) * (
        2.0 * FD
    ) ** (-0.5)


def add_states(earlier_part, later_part):
    return jax.tree.map(
        lambda first_term, second_term: first_term + second_term, earlier_part, later_part
    )


def project(flat_rows, weight_cols, prompts, span, heads, width_last):
    projected = jnp.dot(flat_rows, weight_cols, preferred_element_type=jnp.float32).astype(
        jnp.bfloat16
    )
    return projected.reshape(prompts, span, heads, width_last).astype(jnp.float32)


def body(hidden_in, w_query, w_key, w_value, lengths, owners):
    highest = lax.Precision.HIGHEST
    prompts, span, width = hidden_in.shape
    n_feat = lax.axis_size("feat")
    feat_index = lax.axis_index("feat")
    seq_index = lax.axis_index(SEQ)
    own_heads = H // n_feat
    head_dim = width // H
    flat_rows = hidden_in.reshape(prompts * span, width)
    positions = seq_index * span + jnp.arange(span, dtype=jnp.int32)
    live_mask = (positions[None, :] < lengths[:, None]).astype(jnp.float32)
    key_mask = live_mask[:, :, None, None]
    values_own = jnp.dot(flat_rows, w_value, preferred_element_type=jnp.float32).astype(
        jnp.bfloat16
    )
    value_own = values_own.reshape(prompts, span, own_heads, head_dim).astype(jnp.float32)
    query_cols = lax.dynamic_slice_in_dim(w_query, feat_index * own_heads * FD, own_heads * FD, 1)
    key_cols = lax.dynamic_slice_in_dim(w_key, feat_index * own_heads * FD, own_heads * FD, 1)
    query_own = project(flat_rows, query_cols, prompts, span, own_heads, FD)
    key_own = project(flat_rows, key_cols, prompts, span, own_heads, FD)
    key_quad = quad_features(key_own, key_own) * key_mask
    query_quad = quad_features(query_own, query_own)
    span_quad = jnp.einsum("pchf,pchd->phfd", key_quad, value_own, precision=highest)
    norm_span = jnp.sum(key_quad, axis=1)
    key_low = low_features(key_own) * key_mask
    query_low = low_features(query_own)
    span_low = jnp.einsum("pchf,pchd->phfd", key_low, value_own, precision=highest)
    low_norm = jnp.sum(key_low, axis=1)
    empty_states = (
        jnp.zeros_like(span_quad),
        jnp.zeros_like(norm_span),
        jnp.zeros_like(span_low),
        jnp.zeros_like(low_norm),
    )
    pre_quad, pre_norm, pre_low, pre_lnorm = carried_in(
        (span_quad, norm_span, span_low, low_norm), SEQ, add_states, empty_states
    )
    final_quad, final_norm, final_low, final_lnorm = in_one(
        (span_quad, norm_span, span_low, low_norm), SEQ
    )
    num_low = jnp.einsum("pchf,phfd->pchd", query_low, pre_low, precision=highest)
    den_low = jnp.einsum("pchf,phf->pch", query_low, pre_lnorm, precision=highest)
    num_quad = jnp.einsum("pchf,phfd->pchd", query_quad, pre_quad, precision=highest)
    den_quad = jnp.einsum("pchf,phf->pch", query_quad, pre_norm, precision=highest)
    final_quad, final_norm = (
        lax.all_to_all(
            final_quad.astype(jnp.bfloat16), "feat", split_axis=2, concat_axis=1, tiled=True
        ).astype(final_quad.dtype),
        lax.all_to_all(
            final_norm.astype(jnp.bfloat16), "feat", split_axis=2, concat_axis=1, tiled=True
        ).astype(final_norm.dtype),
    )
    scores = jnp.einsum("pthf,puhf->phtu", query_own, key_own, precision=highest)
    kernel = 1.0 + scores * FD ** (-0.5) + scores * scores * (0.5 / FD)
    causal = (jnp.arange(span)[:, None] >= jnp.arange(span)[None, :]).astype(jnp.float32)
    weight = kernel * causal[None, None, :, :] * live_mask[:, None, None, :]
    num_self = jnp.einsum("phtu,puhd->pthd", weight, value_own, precision=highest)
    den_self = jnp.transpose(jnp.sum(weight, axis=3), (0, 2, 1))
    numerator = num_low + num_quad + num_self
    denominator = den_low + den_quad + den_self
    attended = numerator / denominator[..., None] * live_mask[:, :, None, None]
    squares = jnp.sum(attended * attended, axis=(2, 3))
    sum_squares = lax.psum(squares, "feat")
    scaled = attended * lax.rsqrt(sum_squares / width + NORM_FLOOR)[:, :, None, None]
    mixed = scaled.astype(jnp.bfloat16).reshape(prompts, span, own_heads * head_dim)
    owned = (owners == seq_index).astype(jnp.float32)
    state_quad = (owned[:, None, None, None] * final_quad)[None]
    state_low = (owned[:, None, None, None] * final_low)[None]
    norm_quad = (owned[:, None, None] * final_norm)[None]
    norm_low = (owned[:, None, None] * final_lnorm)[None]
    return (mixed, state_quad, state_low, norm_quad, norm_low)


def solution(mesh):
    torus = Mesh(
        mesh.devices.reshape(8, 4, 2, mesh.shape["feat"]), ("seq_0", "seq_1", "seq_2", "feat")
    )
    placed = (P(None, SEQ, None), P(), P(), P(None, "feat"), P(), P())
    return jax.shard_map(
        body,
        mesh=torus,
        in_specs=placed,
        out_specs=(
            P(None, SEQ, "feat"),
            P(SEQ, None, None, "feat", None),
            P(SEQ, None, "feat", None, None),
            P(SEQ, None, None, "feat"),
            P(SEQ, None, "feat", None),
        ),
        check_vma=False,
    )
```

profile of v0, /device:TPU:1, one launch (start us, length us, event | category | flops | bytes accessed | tf_op | source)
XLA Modules:
  0.0 372.7 jit_solution(8492412542840202425)
XLA Ops:
  8.1 4.2 %fusion.42 = bf16[1024,64]{0,1:T(8,128)(2,1)S(1)} fusion(bf16[1024,2048]{1,0:T(8,128)(2,1)} %bitcast.84, bf16[2048,256]{1,0:T(8,128)(2,1)} %param.8, s32[]{:T(128)S(6)} %select_n.405), kind=kOutput, calls=%fused_computation.60 | convolution fusion | flops 268500992 | bytes 4849668 | tf_op jit(solution)/shard_map/dot_general | solution.py:69
  12.3 0.1 reshape.402
  12.4 4.5 %convolution_convert_fusion = bf16[1024,512]{1,0:T(8,128)(2,1)S(1)} fusion(bf16[1024,2048]{1,0:T(8,128)(2,1)} %bitcast.85, bf16[2048,512]{1,0:T(8,128)(2,1)S(1)} %copy-done), kind=kOutput, calls=%fused_computation.57 | convolution fusion | flops 2148007936 | bytes 7340032 | tf_op jit(solution)/shard_map/dot_general | solution.py:87
  17.0 0.3 reshape.403
  17.3 0.6 copy.97
  17.8 0.1 compare_select_fusion
  17.9 0.7 multiply_reduce_fusion
  18.6 0.7 bitcast_multiply_fusion
  19.4 3.7 fusion.152
  23.1 0.1 compare_convert_fusion
  23.2 0.1 fusion.80
  23.3 0.1 reshape.409
  23.4 0.9 fusion.153
  24.4 0.1 reshape.407
  24.5 19.1 %all-gather.11.cloned.1.call-done = bf16[8,4,256,128]{3,2,1,0:T(8,128)(2,1)} async-done(((bf16[4,4,256,128]{3,2,1,0:T(8,128)(2,1)}), bf16[8,4,256,128]{3,2,1,0:T(8,128)(2,1)}) %all-gather.11.cloned.1.call-update) | async-done | bytes 2097168 | tf_op jit(solution)/shard_map/all_gather | solution.py:27
  43.6 2.8 fusion.44
  46.5 3.2 pad_maximum_fusion
  49.8 49.4 %all-gather.7.cloned.1.call-done = bf16[4,4,4,256,128]{4,3,2,1,0:T(8,128)(2,1)} async-done(((bf16[1,4,4,256,128]{4,3,2,1,0:T(8,128)(2,1)}), bf16[4,4,4,256,128]{4,3,2,1,0:T(8,128)(2,1)}) %all-gather.7.cloned.1.call-update) | async-done | bytes 4194320 | tf_op jit(solution)/shard_map/all_gather | solution.py:27
  99.1 3.9 %fusion.41 = bf16[1,4,4,256,128]{4,3,2,1,0:T(8,128)(2,1)} fusion(bf16[4,4,4,256,128]{4,3,2,1,0:T(8,128)(2,1)} %all-gather.7.cloned.1.call-done), kind=kLoop, calls=%fused_computation.54 | loop fusion | flops 4194304 | bytes 5242880 | tf_op jit(solution)/shard_map/convert_element_type | solution.py:27
  103.1 4.0 %fusion.43 = bf16[1024,64]{0,1:T(8,128)(2,1)S(1)} fusion(bf16[1024,2048]{1,0:T(8,128)(2,1)} %bitcast.86, bf16[2048,256]{1,0:T(8,128)(2,1)S(1)} %copy-done.3, s32[]{:T(128)S(6)} %select_n.405), kind=kOutput, calls=%fused_computation.61 | convolution fusion | flops 268500992 | bytes 4849668 | tf_op jit(solution)/shard_map/dot_general | solution.py:69
  107.1 0.1 reshape.404
  107.2 0.1 convert_element_type.526
  107.3 1.9 all-gather.2
  109.2 9.7 %all_gather.61 = bf16[4,4,4,17]{3,2,1,0:T(4,128)(2,1)S(1)} all-gather(bf16[1,4,4,17]{3,2,1,0:T(4,128)(2,1)S(1)} %fusion.142), channel_id=1, replica_groups=mesh['seq_0'=8,'seq_1'=4,'seq_2'=2,'feat'=4] {'seq_1'}, dimensions={0}, use_global_device_ids=true | all-gather | bytes 2720 | tf_op jit(solution)/shard_map/all_gather | solution.py:27
  118.9 23.0 %all_gather.62 = bf16[8,4,4,17]{3,2,1,0:T(4,128)(2,1)S(1)} all-gather(bf16[1,4,4,17]{3,2,1,0:T(4,128)(2,1)S(1)} %fusion.141), channel_id=1, replica_groups=mesh['seq_0'=8,'seq_1'=4,'seq_2'=2,'feat'=4] {'seq_0'}, dimensions={0}, use_global_device_ids=true | all-gather | bytes 4896 | tf_op jit(solution)/shard_map/all_gather | solution.py:27
  141.9 8.0 %all_gather.63 = bf16[2,4,4,256]{3,2,1,0:T(4,128)(2,1)S(1)} all-gather(bf16[1,4,4,256]{3,2,1,0:T(4,128)(2,1)S(1)} %convert_element_type.526), channel_id=1, replica_groups=mesh['seq_0'=8,'seq_1'=4,'seq_2'=2,'feat'=4] {'seq_2'}, dimensions={0}, use_global_device_ids=true | all-gather | bytes 24576 | tf_op jit(solution)/shard_map/all_gather | solution.py:27
  150.0 10.1 %all_gather.64 = bf16[4,4,4,256]{3,2,1,0:T(4,128)(2,1)S(1)} all-gather(bf16[1,4,4,256]{3,2,1,0:T(4,128)(2,1)S(1)} %fusion.125), channel_id=1, replica_groups=mesh['seq_0'=8,'seq_1'=4,'seq_2'=2,'feat'=4] {'seq_1'}, dimensions={0}, use_global_device_ids=true | all-gather | bytes 40960 | tf_op jit(solution)/shard_map/all_gather | solution.py:27
  160.1 21.9 %all_gather.65 = bf16[8,4,4,256]{3,2,1,0:T(4,128)(2,1)S(1)} all-gather(bf16[1,4,4,256]{3,2,1,0:T(4,128)(2,1)S(1)} %fusion.124), channel_id=1, replica_groups=mesh['seq_0'=8,'seq_1'=4,'seq_2'=2,'feat'=4] {'seq_0'}, dimensions={0}, use_global_device_ids=true | all-gather | bytes 73728 | tf_op jit(solution)/shard_map/all_gather | solution.py:27
  182.0 7.0 %all-gather = bf16[8,4,17,128]{3,1,2,0:T(4,128)(2,1)S(1)} all-gather(bf16[4,4,17,128]{3,1,2,0:T(4,128)(2,1)S(1)} %copy.89), channel_id=2, replica_groups=mesh['seq_0'=8,'seq_1'=4,'seq_2'=2,'feat'=4] {'seq_2'}, dimensions={0}, use_global_device_ids=true | all-gather | bytes 208896 | tf_op jit(solution)/shard_map/all_gather | solution.py:27
  189.0 10.2 %all_gather.54 = bf16[4,4,4,17,128]{4,2,3,1,0:T(4,128)(2,1)S(1)} all-gather(bf16[1,4,4,17,128]{4,2,3,1,0:T(4,128)(2,1)S(1)} %fusion.105), channel_id=1, replica_groups=mesh['seq_0'=8,'seq_1'=4,'seq_2'=2,'feat'=4] {'seq_1'}, dimensions={0}, use_global_device_ids=true | all-gather | bytes 348160 | tf_op jit(solution)/shard_map/all_gather | solution.py:27
  199.3 0.4 fusion.77
  199.8 0.1 fusion.101
  199.8 21.4 %all_gather.55 = bf16[8,4,4,17,128]{4,2,3,1,0:T(4,128)(2,1)S(1)} all-gather(bf16[1,4,4,17,128]{4,2,3,1,0:T(4,128)(2,1)S(1)} %fusion.101), channel_id=1, replica_groups=mesh['seq_0'=8,'seq_1'=4,'seq_2'=2,'feat'=4] {'seq_0'}, dimensions={0}, use_global_device_ids=true | all-gather | bytes 626688 | tf_op jit(solution)/shard_map/all_gather | solution.py:27
  221.2 0.4 fusion.90
  221.6 0.6 multiply_multiply_fusion.1
  222.3 2.1 fusion.122
  224.4 1.5 fusion
  225.9 3.9 %fusion.1 = f32[4,4,128,256]{3,2,1,0:T(8,128)} fusion(bf16[4,256,4,128]{1,3,2,0:T(8,128)(2,1)S(1)} %copy.97, f32[4,4,256,256]{2,3,1,0:T(8,128)S(1)} %get-tuple-element.40, f32[4,256]{1,0:T(4,128)S(1)} %compare_convert_fusion, f32[256,256]{0,1:T(8,128)S(1)} %fusion.82), kind=kOutput, calls=%fused_computation.11 | convolution fusion | flops 1617952768 | bytes 7606272 | tf_op jit(solution)/shard_map/phtu,puhd->pthd/dot_general | solution.py:131
  229.8 83.4 %all-reduce.4.cloned.1.call-done = f32[563472]{0:T(1024)} async-done(((f32[563472]{0:T(1024)}), f32[563472]{0:T(1024)}) %all-reduce.4.cloned.1.call-update) | async-done | bytes 2253904 | tf_op jit(solution)/shard_map/psum | solution.py:46
  313.3 1.7 convert.26
  315.1 0.2 copy.102
  315.3 0.9 reshape.544
  316.2 4.0 %all-to-all-start.1 = ((bf16[4,2,512]{2,1,0:T(2,128)(2,1)}), bf16[4,2,512]{2,1,0:T(2,128)(2,1)S(1)}, u32[]{:S(2)}, u32[]{:S(2)}) async-start(bf16[4,2,512]{2,1,0:T(2,128)(2,1)} %reshape.544), calls=%async_computation.1 | async-start | bytes 16384 | tf_op jit(solution)/shard_map/all_to_all | solution.py:123
  320.3 1.8 copy.99
  322.1 2.3 all-to-all-done.1
  324.4 3.7 %all-to-all-start = ((bf16[4,4,256,128]{3,1,0,2:T(4,128)(2,1)}), bf16[4,4,256,128]{3,1,0,2:T(4,128)(2,1)S(1)}, u32[]{:S(2)}, u32[]{:S(2)}) async-start(bf16[4,4,256,128]{3,1,0,2:T(4,128)(2,1)} %copy.99), calls=%async_computation | async-start | bytes 2097152 | tf_op jit(solution)/shard_map/all_to_all | solution.py:120
  328.1 0.1 reshape.411
  328.3 0.1 broadcast_multiply_fusion.4
  328.3 0.7 copy.106
  329.0 0.7 broadcast_multiply_fusion.6
  329.7 0.6 reshape.545
  330.3 0.2 copy.103
  330.5 0.1 reshape.467
  330.6 0.7 broadcast_multiply_fusion.5
  331.3 7.6 %all-to-all-done = bf16[4,4,256,128]{3,1,0,2:T(4,128)(2,1)S(1)} async-done(((bf16[4,4,256,128]{3,1,0,2:T(4,128)(2,1)}), bf16[4,4,256,128]{3,1,0,2:T(4,128)(2,1)S(1)}, u32[]{:S(2)}, u32[]{:S(2)}) %all-to-all-start) | async-done | bytes 1048608 | tf_op jit(solution)/shard_map/all_to_all | solution.py:120
  338.9 0.3 copy.100
  339.2 0.3 convert_bitcast_fusion
  339.4 0.1 copy.101
  339.6 1.7 broadcast_multiply_fusion.1
  341.3 10.5 %fusion.8 = f32[4,4,128,256]{3,2,1,0:T(8,128)S(1)} fusion(f32[4,256,4,256]{1,3,2,0:T(8,128)} %bitcast.88, bf16[8,4,4,256,128]{4,3,2,1,0:T(8,128)(2,1)} %all-gather.9.cloned.1.call-done, pred[]{:T(512)S(6)} %gt.54, pred[]{:T(512)S(6)} %gt.55, pred[]{:T(512)S(6)} %gt.42, pred[]{:T(512)S(6)} %gt.43, pred[]{:T(512)S(6)} %gt.44, pred[]{:T(512)S(6)} %gt.45, ...), kind=kOutput, calls=%fused_computation.19 | convolution fusion | flops 1632108544 | bytes 20971534 | tf_op jit(solution)/shard_map/pchf,phfd->pchd/dot_general | solution.py:117
  351.9 3.5 multiply_reduce_fusion.1
  355.4 6.8 %psum.14 = f32[4,256]{1,0:T(4,128)S(1)} all-reduce(f32[4,256]{1,0:T(4,128)S(1)} %get-tuple-element.43), channel_id=1, replica_groups=mesh['seq_0'=8,'seq_1'=4,'seq_2'=2,'feat'=4] {'feat'}, use_global_device_ids=true, to_apply=%region_4.5 | all-reduce | flops 1024 | bytes 8192 | tf_op jit(solution)/shard_map/psum | solution.py:137
  362.3 2.0 multiply_convert_fusion
  364.2 1.3 copy.105
  (52 shorter events, 0.8 us)
Async XLA Ops:
  8.0 4.4 %copy-start = (bf16[2048,512]{1,0:T(8,128)(2,1)S(1)}, bf16[2048,512]{1,0:T(8,128)(2,1)}, u32[]{:S(2)}) copy-start(bf16[2048,512]{1,0:T(8,128)(2,1)} %param.9) | copy-start | bytes 6291460
  8.0 35.6 %all-gather.11.cloned.1.call-start = ((), (), s32[]{:S(2)}) async-start(), calls=%async_computation.5 | async-start | bytes 3145728 | tf_op jit(solution)/shard_map/all_gather | solution.py:27
  16.9 0.9 copy-start.4
  23.0 76.1 %all-gather.7.cloned.1.call-start = ((), (), s32[]{:S(2)}) async-start(), calls=%async_computation.2 | async-start | bytes 5242880 | tf_op jit(solution)/shard_map/all_gather | solution.py:27
  46.4 266.8 %all-reduce.4.cloned.1.call-start = ((), (), s32[]{:S(2)}) async-start(), calls=%async_computation.4 | async-start | bytes 4513792 | tf_op jit(solution)/shard_map/psum | solution.py:46
  49.7 53.4 %copy-start.3 = (bf16[2048,256]{1,0:T(8,128)(2,1)S(1)}, bf16[2048,256]{1,0:T(8,128)(2,1)}, u32[]{:S(2)}) copy-start(bf16[2048,256]{1,0:T(8,128)(2,1)} %param.7) | copy-start | bytes 3145732
  49.7 291.6 %all-gather.9.cloned.1.call-start = ((), (), s32[]{:S(2)}) async-start(), calls=%async_computation.3 | async-start | bytes 9437184 | tf_op jit(solution)/shard_map/all_gather | solution.py:27
  222.3 2.1 copy-start.2
  316.2 8.1 %all-to-all-start.1 = ((bf16[4,2,512]{2,1,0:T(2,128)(2,1)}), bf16[4,2,512]{2,1,0:T(2,128)(2,1)S(1)}, u32[]{:S(2)}, u32[]{:S(2)}) async-start(bf16[4,2,512]{2,1,0:T(2,128)(2,1)} %reshape.544), calls=%async_computation.1 | async-start | bytes 16384 | tf_op jit(solution)/shard_map/all_to_all | solution.py:123
  320.3 7.8 %copy-start.5 = (s32[4]{0:T(128)S(1)}, s32[4]{0:T(128)}, u32[]{:S(2)}) copy-start(s32[4]{0:T(128)} %param.11) | copy-start | bytes 52
  320.3 7.8 %slice-start = ((f32[563472]{0:T(1024)}), f32[272]{0:T(512)S(1)}, s32[]{:S(2)}) async-start(f32[563472]{0:T(1024)} %all-reduce.4.cloned.1.call-done), calls=%async_computation.6 | async-start | bytes 4096 | tf_op jit(solution)/shard_map/slice | solution.py:47
  320.3 7.9 %slice-start.1 = ((f32[563472]{0:T(1024)}), f32[34816]{0:T(1024)S(1)}, s32[]{:S(2)}) async-start(f32[563472]{0:T(1024)} %all-reduce.4.cloned.1.call-done), calls=%async_computation.7 | async-start | bytes 278528 | tf_op jit(solution)/shard_map/slice | solution.py:47
  324.4 14.5 %all-to-all-start = ((bf16[4,4,256,128]{3,1,0,2:T(4,128)(2,1)}), bf16[4,4,256,128]{3,1,0,2:T(4,128)(2,1)S(1)}, u32[]{:S(2)}, u32[]{:S(2)}) async-start(bf16[4,4,256,128]{3,1,0,2:T(4,128)(2,1)} %copy.99), calls=%async_computation | async-start | bytes 2097152 | tf_op jit(solution)/shard_map/all_to_all | solution.py:120
  341.3 10.5 %copy-start.6 = (f32[4,4,128,256]{3,2,1,0:T(8,128)S(1)}, f32[4,4,128,256]{3,2,1,0:T(8,128)}, u32[]{:S(2)}) copy-start(f32[4,4,128,256]{3,2,1,0:T(8,128)} %fusion.1) | copy-start | bytes 6291460
  362.3 3.3 copy-start.1
Sparse Core Ops, SparseCore 0:
  23.2 20.4 all-gather.10
  46.6 52.5 all-gather.6
  103.2 97.5 all-gather.8
Sparse Core Ops, SparseCore 1:
  50.4 262.8 all-reduce.3
where the time goes:
time: 379 us; the launch traced here: 373 us
  waiting for transfers between devices  162 us (43%)
  blocking collectives  120 us (32%)
  matrix products  39.3 us (10%)
  other arithmetic  20.1 us (5%)
  between operations  15.7 us (4%)
  starting transfers between devices  7.87 us (2%)
  local copies, waits for them, and re-layouts  7.84 us (2%)
    all_gather x9, blocking collectives, carried_in(): lax.all_gather(part.astype(kind), axis)  113 us
    psum x1, waiting for transfers between devices, in_one(): total = lax.psum(jnp.concatenate([a.ravel() for a in arrays]), axis)  83.4 us
    all_gather x3, waiting for transfers between devices, carried_in(): lax.all_gather(part.astype(kind), axis)  68.5 us
    dot_general x1, matrix products, body(): jnp.einsum('pchf,phfd->pchd', query_quad, pre_quad, precision=highest)  10.5 us
    dot_general x2, matrix products, project(): jnp.dot(flat_rows, weight_cols, preferred_element_type=jnp.float32)  8.19 us
    all_to_all x1, waiting for transfers between devices, body(): lax.all_to_all(final_quad.astype(jnp.bfloat16), 'feat', split_axis=2, con...  7.61 us
  transfers between devices with their start and end apart: 6, of which 5 were waited for; matrix products, arithmetic and copies ran while one was open for 9% of the time, Pallas kernels for 0%

commit v1 on v0

v1 whole, which is shorter than its diff:
```python
import functools

import jax
import jax.numpy as jnp
import numpy as np
from jax import lax
from jax.experimental import pallas as pl
from jax.experimental.pallas import tpu as pltpu
from jax.sharding import Mesh
from jax.sharding import PartitionSpec as P

MESH = pl.DeviceIdType.MESH
F32, BF16 = jnp.float32, jnp.bfloat16
FD = 16
ROWS = 160
LIN, ONE, NORM = 136, 152, 153
HD = 128
NORM_FLOOR = 0.0001
HL = 4
SEQ = ("z", "y", "c")


def packed_pairs():
    pairs = [(i, (i + d) % FD, d) for d in range(8) for i in range(FD)]
    return pairs + [(i, i + 8, 8) for i in range(8)]


def row_of(i, j):
    d = (j - i) % FD
    if d < 8:
        return d * FD + i
    if d == 8:
        return 8 * FD + min(i, j)
    return (FD - d) * FD + j


@functools.cache
def tables(nx):
    ek = np.zeros((2, HL, ROWS, 128), np.float32)
    eq = np.zeros((2, HL, 128, ROWS), np.float32)
    for h in range(HL):
        for r, (i, j, d) in enumerate(packed_pairs()):
            ek[0, h, r, h * FD + i] = ek[1, h, r, h * FD + j] = 1.0
            eq[0, h, h * FD + i, r] = 1.0 / 32 if d == 0 else 1.0 / 16
            eq[1, h, h * FD + j, r] = 1.0
        for i in range(FD):
            ek[0, h, LIN + i, h * FD + i] = ek[1, h, LIN + i, 65] = 1.0
            eq[0, h, h * FD + i, LIN + i] = 0.25
            eq[1, h, 65, LIN + i] = 1.0
        ek[0, h, ONE, 64] = ek[1, h, ONE, 64] = 1.0
        eq[0, h, 65, ONE] = eq[1, h, 65, ONE] = 1.0
    own = FD // nx
    sel = np.zeros((nx, own * FD + 16, ROWS), np.float32)
    for x in range(nx):
        for ii in range(own):
            for j in range(FD):
                sel[x, ii * FD + j, row_of(x * own + ii, j)] = 1.0
        sel[x, own * FD, NORM] = sel[x, own * FD + 1, NORM + 1] = 1.0
    return (
        ek.reshape(2 * HL * ROWS, 128).astype(BF16),
        eq.reshape(2 * HL, 128, ROWS).astype(BF16),
        sel.reshape(-1, ROWS).astype(BF16),
    )


def dot(a, b, ca=1, cb=0):
    return lax.dot_general(a, b, (((ca,), (cb,)), ((), ())), preferred_element_type=F32)


def kernel(
    sizes, len_ref, hid_hbm, wv_hbm, wk_hbm, wq_hbm, ek_hbm, eq_hbm, sel_hbm, mixed_hbm, fx_hbm, low_hbm,
    hid, wv, wkq, ek, eq, sel, val, keyt, qry, phi, nself, dself, att, mixed, cm, sq, rsq,
    loc, r0, csum, ry, tz, rz, pz, rpz, tt, rtt, py, rpy, pc, rpc, fxs, fxa, lowa,
    lsem, hsem, s0, v0, sy, vy, sz, vz, sz2, vz2, sz3, vz3, sy2, vy2, s02, v02,
    sx, vx, sy3, vy3, sy4, vy4, s3, v3, sx2, vx2, osem,
):
    nz, ny, nc, nx, span, width = sizes
    zr = 2 * ROWS // nz
    z, y, c, x = (lax.axis_index(a) for a in ("z", "y", "c", "x"))
    other = 1 - c
    pos0 = ((z * ny + y) * nc + c) * span

    col = pl.multiple_of((x * (HL * FD)) // 128 * 128, 128)
    shift = lax.rem(x * (HL * FD), 128)

    def hid_copy(p):
        return pltpu.make_async_copy(hid_hbm.at[p], hid.at[p], hsem.at[p])

    loads = [
        pltpu.make_async_copy(wk_hbm.at[:, pl.ds(col, 128)], wkq.at[:, pl.ds(0, 128)], lsem.at[0]),
        pltpu.make_async_copy(wq_hbm.at[:, pl.ds(col, 128)], wkq.at[:, pl.ds(128, 128)], lsem.at[1]),
        pltpu.make_async_copy(wv_hbm, wv, lsem.at[2]),
        pltpu.make_async_copy(ek_hbm, ek, lsem.at[3]),
        pltpu.make_async_copy(eq_hbm, eq, lsem.at[4]),
        pltpu.make_async_copy(sel_hbm, sel, lsem.at[5]),
    ]
    loads[0].start()
    loads[1].start()
    hid_copy(lax.rem(y + 1, ny)).start()
    loads[2].start()
    loads[3].start()
    for s in range(1, ny):
        hid_copy(lax.rem(y + 1 + s, ny)).start()
    loads[4].start()
    loads[5].start()

    barrier = pltpu.get_barrier_semaphore()
    peers = [(z, y, other, x)]
    peers += [(z, lax.rem(y + d, ny), c, x) for d in range(1, ny)]
    peers += [(lax.rem(z + d, nz), y, c, x) for d in range(1, nz)]
    peers += [(z, y, c, lax.rem(x + d, nx)) for d in range(1, nx)]
    for peer in peers:
        pl.semaphore_signal(barrier, inc=1, device_id=peer, device_id_type=MESH)
    pl.semaphore_wait(barrier, len(peers))

    def remote(src, dst, send, recv, dev):
        return pltpu.make_async_remote_copy(
            src_ref=src, dst_ref=dst, send_sem=send, recv_sem=recv, device_id=dev, device_id_type=MESH
        )

    core = (z, y, other, x)

    def at_y(q):
        return (z, q, c, x)

    def at_z(q):
        return (q, y, c, x)

    def at_x(q):
        return (z, y, c, q)

    for load in loads[:4]:
        load.wait()
    ones = jnp.ones((8, span), BF16)

    def to_core(p):
        return remote(loc.at[p, other], r0.at[p], s0.at[p], v0.at[p], core)

    def chip_sum(p):
        to_core(p).wait_recv()
        csum[p] = (loc[p, c].astype(F32) + r0[p].astype(F32)).astype(BF16)

    def sum_to_y(p):
        return remote(csum.at[p], ry.at[y], sy.at[p], vy.at[y], at_y(p))

    def state(s, carry):
        p = lax.rem(y + 1 + s, ny)
        hid_copy(p).wait()
        rows = hid[p]
        kq = dot(rows, wkq[...])
        k = pltpu.roll(kq[:, :128], shift, 1).astype(BF16).astype(F32)
        q = pltpu.roll(kq[:, 128:], shift, 1)
        lane = lax.broadcasted_iota(jnp.int32, (span, 128), 1)
        qry[p] = jnp.where(lane < 64, q, jnp.where(lane == 65, 1.0, 0.0)).astype(BF16)
        kt = jnp.transpose(k)
        row = lax.broadcasted_iota(jnp.int32, (128, span), 0)
        live = (lax.broadcasted_iota(jnp.int32, (128, span), 1) + pos0 < len_ref[p]).astype(F32)
        kt = jnp.where(row < 64, kt, jnp.where(row == 64, 1.0, 0.0)) * live + jnp.where(row == 65, 1.0, 0.0)
        kt = kt.astype(BF16)
        keyt[p] = kt
        val[p] = dot(rows, wv[...]).astype(BF16)
        for h in range(HL):
            left = dot(ek[h * ROWS : (h + 1) * ROWS], kt)
            right = dot(ek[(HL + h) * ROWS : (HL + h + 1) * ROWS], kt)
            feat = (left * right).astype(BF16)
            st = dot(feat, val[p, :, h * HD : (h + 1) * HD])
            zn = dot(ones, feat, 1, 1)
            first = zn[:, :128]
            rest = jnp.concatenate([zn[:, 128:], jnp.zeros((8, 256 - ROWS), F32)], axis=1)
            sub = lax.broadcasted_iota(jnp.int32, (8, 128), 0)
            tail = jnp.where(sub == 1, first, jnp.where(sub == 2, rest, st[ROWS - 8 :]))
            loc[p, h // 2, h % 2] = jnp.concatenate([st[: ROWS - 8], tail], axis=0).astype(BF16)
        to_core(p).start()

        @pl.when(s > 0)
        def _():
            before = lax.rem(y + s, ny)
            chip_sum(before)
            sum_to_y(before).start()

        return carry

    lax.fori_loop(0, ny, state, 0)

    chip_sum(y)
    ry[y] = csum[y]
    for d in range(1, ny):
        q = lax.rem(y + d, ny)
        remote(csum.at[q], ry.at[q], sy.at[q], vy.at[q], at_y(q)).wait_recv()
    total = ry[0].astype(F32)
    for q in range(1, ny):
        total = total + ry[q].astype(F32)
    total = total.reshape(2 * ROWS, HD)
    for q in range(nz):
        tz[q] = total[q * zr : (q + 1) * zr].astype(BF16)

    def slice_to_z(q):
        return remote(tz.at[q], rz.at[z], sz.at[q], vz.at[z], at_z(q))

    for d in range(1, nz):
        slice_to_z(lax.rem(z + d, nz)).start()
    rz[z] = tz[z]

    for load in loads[4:]:
        load.wait()

    def inside(p):
        q = qry[p]
        t_at = lax.broadcasted_iota(jnp.int32, (span, span), 0)
        u_at = lax.broadcasted_iota(jnp.int32, (span, span), 1)
        seen = (u_at <= t_at) & (u_at + pos0 < len_ref[p])
        row = lax.broadcasted_iota(jnp.int32, (128, span), 0)
        kt = keyt[p]
        for h in range(HL):
            phi[p, h] = (dot(q, eq[h]) * dot(q, eq[HL + h])).astype(BF16)
            mine = jnp.where((row >= h * FD) & (row < (h + 1) * FD), kt, jnp.zeros_like(kt))
            half = dot(q, mine) * 0.25 + 1.0
            weight = jnp.where(seen, half * half * 0.5 + 0.5, 0.0).astype(BF16)
            nself[p, h] = dot(weight, val[p, :, h * HD : (h + 1) * HD])
            dself[p, h] = dot(weight, jnp.ones((span, HD), BF16))

    def inside_step(p, carry):
        inside(p)
        return carry

    lax.fori_loop(0, ny // 2, inside_step, 0)

    for d in range(1, nz):
        q = lax.rem(z + d, nz)
        remote(tz.at[q], rz.at[q], sz.at[q], vz.at[q], at_z(q)).wait_recv()
    run = jnp.zeros((zr, HD), F32)
    for q in range(nz):
        pz[q] = run.astype(BF16)
        run = run + rz[q].astype(F32)
    tt[...] = run.astype(BF16)

    def prefix_to_z(q):
        return remote(pz.at[q], rpz.at[z], sz2.at[q], vz2.at[z], at_z(q))

    def total_to_z(q):
        return remote(tt, rtt.at[z], sz3.at[q], vz3.at[z], at_z(q))

    for d in range(1, nz):
        prefix_to_z(lax.rem(z + d, nz)).start()
    rpz[z] = pz[z]
    for d in range(1, nz):
        total_to_z(lax.rem(z + d, nz)).start()
    rtt[z] = tt[...]

    lax.fori_loop(ny // 2, ny, inside_step, 0)

    for d in range(1, nz):
        q = lax.rem(z + d, nz)
        remote(pz.at[q], rpz.at[q], sz2.at[q], vz2.at[q], at_z(q)).wait_recv()
    run = jnp.concatenate([rpz[q].astype(F32) for q in range(nz)], axis=0).reshape(2, ROWS, HD)
    for q in range(ny):
        py[q] = run.astype(BF16)
        run = run + ry[q].astype(F32)

    def prefix_to_y(q):
        return remote(py.at[q], rpy.at[y], sy2.at[q], vy2.at[y], at_y(q))

    for d in range(1, ny):
        prefix_to_y(lax.rem(y + d, ny)).start()
    rpy[y] = py[y]

    part = sel.shape[0] // nx
    for d in range(1, nz):
        q = lax.rem(z + d, nz)
        remote(tt, rtt.at[q], sz3.at[q], vz3.at[q], at_z(q)).wait_recv()
    whole = jnp.concatenate([rtt[q].astype(F32) for q in range(nz)], axis=0).reshape(2, ROWS, HD).astype(BF16)
    for i in range(2):
        picked = dot(sel[...], whole[i]).astype(BF16)
        for q in range(nx):
            fxs[q, i] = picked[q * part : (q + 1) * part]
        lowa[c, y, i] = whole[i, 128:]

    def final_to_x(q):
        return remote(fxs.at[q], fxa.at[c, y, x], sx.at[q], vx.at[x], at_x(q))

    for d in range(1, nx):
        final_to_x(lax.rem(x + d, nx)).start()
    fxa[c, y, x] = fxs[x]

    def attend(p, h, state):
        tail = state[ROWS - 8 :]
        norm = jnp.concatenate(
            [jnp.broadcast_to(tail[1:2], (HD, HD)), jnp.broadcast_to(tail[2:3, : ROWS - HD], (HD, ROWS - HD))], axis=1
        ).astype(BF16)
        feats = phi[p, h]
        num = dot(feats, state.astype(BF16)) + nself[p, h]
        den = dot(feats, norm, 1, 1) + dself[p, h]
        live = lax.broadcasted_iota(jnp.int32, (span, HD), 0) + pos0 < len_ref[p]
        att[p, h] = jnp.where(live, num / den, 0.0)

    def to_core2(p):
        return remote(pc.at[p], rpc.at[p], s02.at[p], v02.at[p], core)

    at_one = (c == 1).astype(F32)

    def near(s, carry):
        p = lax.rem(y + s, ny)

        @pl.when(s > 0)
        def _():
            remote(py.at[p], rpy.at[p], sy2.at[p], vy2.at[p], at_y(p)).wait_recv()

        chip = rpy[p].astype(F32)
        pc[p] = (chip + (1.0 - at_one) * loc[p, c].astype(F32)).astype(BF16)
        to_core2(p).start()
        mine = chip + at_one * r0[p].astype(F32)
        for i in range(2):
            attend(p, c * 2 + i, mine[i])
        return carry

    lax.fori_loop(0, ny, near, 0)

    for d in range(1, nx):
        q = lax.rem(x + d, nx)
        remote(fxs.at[q], fxa.at[c, y, q], sx.at[q], vx.at[q], at_x(q)).wait_recv()

    def final_to_y(q):
        return remote(fxa.at[c, y], fxa.at[c, y], sy3.at[q], vy3.at[y], at_y(q))

    def low_to_y(q):
        return remote(lowa.at[c, y], lowa.at[c, y], sy4.at[q], vy4.at[y], at_y(q))

    for d in range(1, ny):
        q = lax.rem(y + d, ny)
        final_to_y(q).start()
        low_to_y(q).start()

    def far(s, carry):
        p = lax.rem(y + s, ny)
        to_core2(p).wait_recv()
        there = rpc[p].astype(F32)
        for i in range(2):
            attend(p, other * 2 + i, there[i])
        square = att[p, 0] * att[p, 0]
        for h in range(1, HL):
            square = square + att[p, h] * att[p, h]
        high = square.astype(BF16)
        rest = (square - high.astype(F32)).astype(BF16)
        unit = jnp.ones((8, HD), BF16)
        sq[p] = dot(unit, high, 1, 1) + dot(unit, rest, 1, 1)
        return carry

    lax.fori_loop(0, ny, far, 0)

    def square_to_x(q):
        return remote(sq, rsq.at[x], sx2.at[q], vx2.at[x], at_x(q))

    for d in range(1, nx):
        square_to_x(lax.rem(x + d, nx)).start()

    for d in range(1, ny):
        q = lax.rem(y + d, ny)
        remote(fxa.at[c, y], fxa.at[c, q], sy3.at[q], vy3.at[q], at_y(q)).wait_recv()
        remote(lowa.at[c, y], lowa.at[c, q], sy4.at[q], vy4.at[q], at_y(q)).wait_recv()
    final_to_core = remote(fxa.at[c], fxa.at[c], s3.at[0], v3.at[0], core)
    low_to_core = remote(lowa.at[c], lowa.at[c], s3.at[1], v3.at[1], core)
    final_to_core.start()
    low_to_core.start()

    rsq[x] = sq[...]
    for d in range(1, nx):
        q = lax.rem(x + d, nx)
        remote(sq, rsq.at[q], sx2.at[q], vx2.at[q], at_x(q)).wait_recv()

    def out_copy(p):
        return pltpu.make_async_copy(mixed.at[p], mixed_hbm.at[p], osem.at[p])

    def scale(p, carry):
        squares = rsq[0, p]
        for q in range(1, nx):
            squares = squares + rsq[q, p]
        factor = lax.rsqrt(squares / width + NORM_FLOOR)
        cm[...] = jnp.transpose(factor)
        factor = jnp.broadcast_to(cm[:, 0:1], (span, HD))
        for h in range(HL):
            mixed[p, :, h * HD : (h + 1) * HD] = (att[p, h] * factor).astype(BF16)
        out_copy(p).start()
        return carry

    lax.fori_loop(0, ny, scale, 0)

    remote(fxa.at[c], fxa.at[other], s3.at[0], v3.at[0], core).wait_recv()
    remote(lowa.at[c], lowa.at[other], s3.at[1], v3.at[1], core).wait_recv()
    outs = [
        pltpu.make_async_copy(fxa, fx_hbm, osem.at[ny]),
        pltpu.make_async_copy(lowa, low_hbm, osem.at[ny + 1]),
    ]
    for out in outs:
        out.start()

    for p in range(ny):
        to_core(p).wait_send()
        to_core2(p).wait_send()
    for d in range(1, ny):
        q = lax.rem(y + d, ny)
        sum_to_y(q).wait_send()
        prefix_to_y(q).wait_send()
        final_to_y(q).wait_send()
        low_to_y(q).wait_send()
    for d in range(1, nz):
        q = lax.rem(z + d, nz)
        slice_to_z(q).wait_send()
        prefix_to_z(q).wait_send()
        total_to_z(q).wait_send()
    for d in range(1, nx):
        q = lax.rem(x + d, nx)
        final_to_x(q).wait_send()
        square_to_x(q).wait_send()
    final_to_core.wait_send()
    low_to_core.wait_send()
    for p in range(ny):
        out_copy(p).wait()
    for out in outs:
        out.wait()


def body(hidden_in, w_query, w_key, w_value, lengths, owners):
    nz, ny, nc, nx = (lax.axis_size(a) for a in ("z", "y", "c", "x"))
    prompts, span, width = hidden_in.shape
    own = FD // nx * FD
    part = own + 16
    zr = 2 * ROWS // nz
    ek, eq, sel = (jnp.asarray(t) for t in tables(nx))
    anyspace = pl.BlockSpec(memory_space=pl.ANY)
    dma = pltpu.SemaphoreType.DMA

    def vmem(*shape, kind=BF16):
        return pltpu.VMEM(shape, kind)

    block = (2, ROWS, HD)
    mixed, fx, low = pl.pallas_call(
        functools.partial(kernel, (nz, ny, nc, nx, span, HD * HL * nx)),
        out_shape=(
            jax.ShapeDtypeStruct((prompts, span, HL * HD), BF16),
            jax.ShapeDtypeStruct((nc, prompts, nx, 2, part, HD), BF16),
            jax.ShapeDtypeStruct((nc, prompts, 2, ROWS - 128, HD), BF16),
        ),
        in_specs=[pl.BlockSpec(memory_space=pltpu.SMEM)] + [anyspace] * 7,
        out_specs=(anyspace,) * 3,
        scratch_shapes=[
            vmem(prompts, span, width), vmem(width, HL * HD), vmem(width, 256),
            vmem(*ek.shape), vmem(*eq.shape), vmem(*sel.shape),
            vmem(prompts, span, HL * HD), vmem(prompts, 128, span), vmem(prompts, span, 128),
            vmem(prompts, HL, span, ROWS),
            vmem(prompts, HL, span, HD, kind=F32), vmem(prompts, HL, span, HD, kind=F32),
            vmem(prompts, HL, span, HD, kind=F32),
            vmem(prompts, span, HL * HD), vmem(span, 8, kind=F32),
            vmem(prompts, 8, span, kind=F32), vmem(nx, prompts, 8, span, kind=F32),
            vmem(prompts, 2, *block), vmem(prompts, *block), vmem(prompts, *block), vmem(ny, *block),
            vmem(nz, zr, HD), vmem(nz, zr, HD), vmem(nz, zr, HD), vmem(nz, zr, HD), vmem(zr, HD), vmem(nz, zr, HD),
            vmem(ny, *block), vmem(prompts, *block), vmem(prompts, *block), vmem(prompts, *block),
            vmem(nx, 2, part, HD), vmem(nc, prompts, nx, 2, part, HD), vmem(nc, prompts, 2, ROWS - 128, HD),
            dma((6,)), dma((prompts,)), dma((prompts,)), dma((prompts,)),
            dma((ny,)), dma((ny,)), dma((nz,)), dma((nz,)), dma((nz,)), dma((nz,)), dma((nz,)), dma((nz,)),
            dma((ny,)), dma((ny,)), dma((prompts,)), dma((prompts,)),
            dma((nx,)), dma((nx,)), dma((ny,)), dma((ny,)), dma((ny,)), dma((ny,)), dma((2,)), dma((2,)),
            dma((nx,)), dma((nx,)), dma((prompts + 2,)),
        ],
        compiler_params=pltpu.CompilerParams(
            collective_id=0, has_side_effects=True, vmem_limit_bytes=60 * 1024 * 1024
        ),
        name="prefill",
    )(lengths, hidden_in, w_value, w_key, w_query, ek, eq, sel)

    owned = owners == lax.axis_index(SEQ)
    fx = jnp.transpose(fx, (1, 2, 0, 3, 4, 5)).reshape(prompts, HL * nx, part, HD)
    low = jnp.transpose(low, (1, 0, 2, 3, 4)).reshape(prompts, HL, ROWS - 128, HD)
    quad_scale = (2.0 * FD) ** (-0.5)
    low_scale = FD ** (-0.25)
    state_quad = jnp.where(owned[:, None, None, None], fx[:, :, :own].astype(F32) * quad_scale, 0.0)[None]
    norms = jnp.concatenate([fx[:, :, own], fx[:, :, own + 1, : ROWS - 128]], axis=-1)
    pick = lax.dynamic_slice_in_dim(sel, lax.axis_index("x") * part, own, 0)
    norm_quad = dot(norms.reshape(prompts * HL * nx, ROWS), pick, 1, 1).reshape(prompts, HL * nx, own)
    norm_quad = jnp.where(owned[:, None, None], norm_quad * quad_scale, 0.0)[None]
    lin, one = LIN - 128, ONE - 128
    state_low = jnp.concatenate(
        [low[:, :, one : one + 1].astype(F32), low[:, :, lin : lin + FD].astype(F32) * low_scale], axis=2
    )
    state_low = jnp.where(owned[:, None, None, None], state_low, 0.0)[None]
    rest = low[:, :, NORM + 1 - 128].astype(F32)
    norm_low = jnp.concatenate([rest[..., one : one + 1], rest[..., lin : lin + FD] * low_scale], axis=-1)
    norm_low = jnp.where(owned[:, None, None], norm_low, 0.0)[None]
    return mixed, state_quad, state_low, norm_quad, norm_low


def torus_of(mesh, shape=(8, 4, 2, 4)):
    return Mesh(mesh.devices.reshape(shape), ("z", "y", "c", "x"))


def run_on(torus):
    return jax.shard_map(
        body,
        mesh=torus,
        in_specs=(P(None, SEQ, None), P(), P(), P(None, "x"), P(), P()),
        out_specs=(
            P(None, SEQ, "x"),
            P(SEQ, None, None, "x", None),
            P(SEQ, None, "x", None, None),
            P(SEQ, None, None, "x"),
            P(SEQ, None, "x", None),
        ),
        check_vma=False,
    )


def solution(mesh):
    ny, nc = 4, 2
    feat = mesh.shape["feat"]
    return run_on(torus_of(mesh, (mesh.shape["seq"] // (ny * nc), ny, nc, feat)))
```

time: 379 us -> 59.6 us (0.16); the launches traced: 373 us -> 59.4 us
  waiting for transfers between devices: 162 us -> 0 us
  blocking collectives: 120 us -> 0 us
  Pallas kernels: 0 us -> 50.6 us
  matrix products: 39.3 us -> 1.52 us
  other arithmetic: 20.1 us -> 3.24 us
  between operations: 15.7 us -> 0.73 us
  starting transfers between devices: 7.87 us -> 0 us
  local copies, waits for them, and re-layouts: 7.84 us -> 3.3 us
    all_gather x9 -> x0, blocking collectives: 113 us -> none  [carried_in(): lax.all_gather(part.astype(kind), axis)]
    psum x1 -> x0, waiting for transfers between devices: 83.4 us -> none  [in_one(): total = lax.psum(jnp.concatenate([a.ravel() for a in arrays]), axis)]
    all_gather x3 -> x0, waiting for transfers between devices: 68.5 us -> none  [carried_in(): lax.all_gather(part.astype(kind), axis)]
    pallas_call x0 -> x1, Pallas kernels: none -> 50.6 us  [body(): pl.pallas_call(functools.partial(kernel, (nz, ny, nc, nx, span, HD * HL *...]
    dot_general x11 -> x1, matrix products: 39.3 us -> 1.52 us  [dot(): lax.dot_general(a, b, (((ca,), (cb,)), ((), ())), preferred_element_type=...]
    all_to_all x2 -> x0, waiting for transfers between devices: 9.88 us -> none  [the longest x1 7.61 us: body(): lax.all_to_all(final_quad.astype(jnp.bfloat16), 'feat', split_axis=2, con...]
    convert_element_type x17 -> x1, other arithmetic: 9.17 us -> 0.01 us  [body(): rest = low[:, :, NORM + 1 - 128].astype(F32)]
    all_to_all x2 -> x0, starting transfers between devices: 7.71 us -> none  [the longest x1 3.97 us: body(): lax.all_to_all(final_norm.astype(jnp.bfloat16), 'feat', split_axis=2, con...]
  transfers between devices with their start and end apart: 6 -> 0, of which waited for: 5 -> 0; matrix products, arithmetic and copies ran while one was open for 9% -> 0% of each run, Pallas kernels for 0% -> 0%
where the time goes in v1:
time: 59.6 us; the launch traced here: 59.4 us
  Pallas kernels  50.6 us (85%)
  local copies, waits for them, and re-layouts  3.3 us (6%)
  other arithmetic  3.24 us (5%)
  matrix products  1.52 us (3%)
  between operations  0.73 us (1%)
    pallas_call x1, Pallas kernels, body(): pl.pallas_call(functools.partial(kernel, (nz, ny, nc, nx, span, HD * HL *...  50.6 us
    broadcast_in_dim x1, other arithmetic, body(): jnp.where(owned[:, None, None, None], fx[:, :, :own].astype(F32) * quad_s...  1.71 us
    unnamed x8, local copies, waits for them, and re-layouts  1.68 us
    dot_general x1, matrix products, dot(): lax.dot_general(a, b, (((ca,), (cb,)), ((), ())), preferred_element_type=...  1.52 us
    transpose x1, local copies, waits for them, and re-layouts, body(): jnp.transpose(fx, (1, 2, 0, 3, 4, 5)).reshape(prompts, HL * nx, part, HD)  1.48 us

profile of v1, /device:TPU:1, one launch (start us, length us, event | category | flops | bytes accessed | tf_op | source)
XLA Modules:
  0.0 59.4 jit_solution(1045773748107236067)
XLA Ops:
  0.6 0.7 %broadcast_compare_fusion = pred[4]{0:T(512)(128)(4,1)S(1)} fusion(s32[4]{0:T(128)} %param.14, s32[]{:T(128)S(6)} %add.10), kind=kLoop, calls=%fused_computation.20 | loop fusion | flops 4 | bytes 24 | tf_op jit(solution)/shard_map/eq | solution.py:470
  1.3 50.6 %prefill.1 = (bf16[4,256,512]{2,1,0:T(8,128)(2,1)}, bf16[2,4,4,2,80,128]{5,4,3,2,1,0:T(8,128)(2,1)}, bf16[2,4,2,32,128]{4,3,2,1,0:T(8,128)(2,1)}) custom-call(s32[4]{0:T(128)} %len_ref.1, bf16[4,256,2048]{2,1,0:T(8,128)(2,1)} %hid_hbm.1, bf16[2048,512]{1,0:T(8,128)(2,1)} %wv_hbm.1, bf16[2048,256]{1,0:T(8,128)(2,1)} %wk_hbm.1, bf16[2048,256]{1,0:T(8,128)(2,1)} %wq_hbm.1, ...), custom_call_target="tpu_custom_call" | custom-call | tf_op jit(solution)/shard_map/prefill/pallas_call | solution.py:436
  51.9 0.0 copy-start.1
  51.9 1.5 %copy.17 = bf16[4,4,2,2,80,128]{5,4,3,2,1,0:T(8,128)(2,1)S(1)} copy(bf16[4,4,2,2,80,128]{5,4,3,1,0,2:T(8,128)(2,1)} %bitcast.28) | data formatting | bytes 2621440 | tf_op jit(solution)/shard_map/transpose | solution.py:471
  53.5 1.5 %fusion.1 = f32[1,4,16,64]{3,2,1,0:T(8,128)} fusion(bf16[4,16,32]{2,1,0:T(8,128)(2,1)S(1)} %bitcast.35, bf16[4,16,128]{2,1,0:T(8,128)(2,1)S(1)} %bitcast.34, bf16[320,160]{1,0:T(8,128)(2,1)} %constant.43.clone.sel_hbm, s32[]{:T(128)S(6)} %select_n.35, pred[4]{0:T(512)(128)(4,1)S(1)} %broadcast_compare_fusion), kind=kOutput, calls=%fused_computation.3 | convolution fusion | flops 1359872 | bytes 69640 | tf_op jit(solution)/shard_map/dot_general | solution.py:67
  55.0 0.0 copy-done.1
  55.0 0.0 copy-start
  55.1 0.1 fusion.7
  55.1 0.1 slice_bitcast_fusion
  55.2 0.7 %maximum_select_fusion.1 = f32[1,4,4,17]{3,2,1,0:T(4,128)} fusion(f32[1,4,4,16]{3,2,1,0:T(4,128)S(1)} %fusion.7, f32[1,4,4,1]{3,2,1,0:T(4,128)S(1)} %slice_bitcast_fusion, pred[4]{0:T(512)(128)(4,1)S(1)} %broadcast_compare_fusion), kind=kLoop, calls=%fused_computation.17 | loop fusion | flops 544 | bytes 2180 | tf_op jit(solution)/shard_map/jit(_where)/select_n | solution.py:487
  55.9 0.1 maximum_select_fusion
  56.0 0.7 %copy.23 = f32[1,4,4,17,128]{4,2,3,1,0:T(4,128)} copy(f32[1,4,4,17,128]{4,3,2,1,0:T(8,128)S(1)} %maximum_select_fusion) | data formatting | bytes 278528
  56.7 1.7 %select_bitcast_fusion = f32[1,4,16,64,128]{4,3,2,1,0:T(8,128)} fusion(bf16[4,16,80,128]{3,2,1,0:T(8,128)(2,1)S(1)} %bitcast.27, pred[4]{0:T(512)(128)(4,1)S(1)} %broadcast_compare_fusion), kind=kLoop, calls=%fused_computation | loop fusion | flops 1572864 | bytes 3145732 | tf_op jit(solution)/shard_map/broadcast_in_dim | solution.py:475
  58.4 0.0 copy-done
  58.4 1.0 %copy.33 = bf16[4,256,512]{2,1,0:T(8,128)(2,1)} copy(bf16[4,256,512]{2,1,0:T(8,128)(2,1)S(1)} %copy-done) | data formatting | bytes 2097152
  (8 shorter events, 0.1 us)
Async XLA Ops:
  51.9 3.1 %copy-start.1 = (bf16[2,4,2,32,128]{4,3,2,1,0:T(8,128)(2,1)S(1)}, bf16[2,4,2,32,128]{4,3,2,1,0:T(8,128)(2,1)}, u32[]{:S(2)}) copy-start(bf16[2,4,2,32,128]{4,3,2,1,0:T(8,128)(2,1)} %get-tuple-element.10) | copy-start | bytes 393220
  55.0 3.4 %copy-start = (bf16[4,256,512]{2,1,0:T(8,128)(2,1)S(1)}, bf16[4,256,512]{2,1,0:T(8,128)(2,1)}, u32[]{:S(2)}) copy-start(bf16[4,256,512]{2,1,0:T(8,128)(2,1)} %get-tuple-element.28) | copy-start | bytes 3145732

commit v2 on v1

v2 whole, which is shorter than its diff:
```python
import functools

import jax
import jax.numpy as jnp
import numpy as np
from jax import lax
from jax.experimental import pallas as pl
from jax.experimental.pallas import tpu as pltpu
from jax.sharding import Mesh
from jax.sharding import PartitionSpec as P

MESH = pl.DeviceIdType.MESH
F32, BF16 = jnp.float32, jnp.bfloat16
FD = 16
ROWS = 160
LIN, ONE, NORM = 136, 152, 153
HD = 128
NORM_FLOOR = 0.0001
HL = 4
SEQ = ("z", "y", "c")


def packed_pairs():
    pairs = [(i, (i + d) % FD, d) for d in range(8) for i in range(FD)]
    return pairs + [(i, i + 8, 8) for i in range(8)]


def row_of(i, j):
    d = (j - i) % FD
    if d < 8:
        return d * FD + i
    if d == 8:
        return 8 * FD + min(i, j)
    return (FD - d) * FD + j


@functools.cache
def tables(nx):
    eq = np.zeros((2, HL, 128, ROWS), np.float32)
    for h in range(HL):
        for r, (i, j, d) in enumerate(packed_pairs()):
            eq[0, h, h * FD + i, r] = 1.0 / 32 if d == 0 else 1.0 / 16
            eq[1, h, h * FD + j, r] = 1.0
        for i in range(FD):
            eq[0, h, h * FD + i, LIN + i] = 0.25
            eq[1, h, 65, LIN + i] = 1.0
        eq[0, h, 65, ONE] = eq[1, h, 65, ONE] = 1.0
    own = FD // nx
    sel = np.zeros((nx, own * FD, ROWS), np.float32)
    for x in range(nx):
        for ii in range(own):
            for j in range(FD):
                sel[x, ii * FD + j, row_of(x * own + ii, j)] = 1.0
    return (
        eq.reshape(2 * HL, 128, ROWS).astype(BF16),
        sel.reshape(-1, ROWS).astype(BF16),
    )


def dot(a, b, ca=1, cb=0):
    return lax.dot_general(a, b, (((ca,), (cb,)), ((), ())), preferred_element_type=F32)


def kernel(
    sizes, len_ref, hid_hbm, wv_hbm, wk_hbm, wq_hbm, eq_hbm, sel_hbm, mixed_hbm, fx_hbm, low_hbm,
    hid, wv, wk, wkt, wq, eq, sel, val, keyt, kd, phi, nself, dself, att, mixed, sq, rsq,
    loc, r0, csum, ry, tz, rz, pz, rpz, tt, rtt, py, rpy, pc, rpc, fxs, fxa, lowa,
    lsem, hsem, s0, v0, sy, vy, sz, vz, sz2, vz2, sz3, vz3, sy2, vy2, s02, v02,
    sx, vx, sy3, vy3, sy4, vy4, s3, v3, s4, v4, sx2, vx2, osem,
):
    nz, ny, nc, nx, span, width = sizes
    width_in = wk.shape[0]
    zr = 2 * ROWS // nz
    z, y, c, x = (lax.axis_index(a) for a in ("z", "y", "c", "x"))
    other = 1 - c
    pos0 = ((z * ny + y) * nc + c) * span

    col = pl.multiple_of((x * (HL * FD)) // 128 * 128, 128)
    shift = lax.rem(x * (HL * FD), 128)

    def turn(s):
        return lax.rem(y + jnp.where(s == 0, 2, jnp.where(s == 1, 1, jnp.where(s == 2, 3, 0))), ny)

    def hid_copy(p):
        return pltpu.make_async_copy(hid_hbm.at[p], hid.at[p], hsem.at[p])

    loads = [
        pltpu.make_async_copy(wk_hbm.at[:, pl.ds(col, 128)], wk, lsem.at[0]),
        pltpu.make_async_copy(wv_hbm, wv, lsem.at[1]),
        pltpu.make_async_copy(wq_hbm.at[:, pl.ds(col, 128)], wq, lsem.at[2]),
        pltpu.make_async_copy(eq_hbm, eq, lsem.at[3]),
        pltpu.make_async_copy(sel_hbm, sel, lsem.at[4]),
    ]
    loads[0].start()
    hid_copy(turn(0)).start()
    loads[1].start()
    for s in range(1, ny):
        hid_copy(turn(s)).start()
    for load in loads[2:]:
        load.start()

    barrier = pltpu.get_barrier_semaphore()
    peers = [(z, y, other, x)]
    peers += [(z, lax.rem(y + d, ny), c, x) for d in range(1, ny)]
    peers += [(lax.rem(z + d, nz), y, c, x) for d in range(1, nz)]
    peers += [(z, y, c, lax.rem(x + d, nx)) for d in range(1, nx)]
    for peer in peers:
        pl.semaphore_signal(barrier, inc=1, device_id=peer, device_id_type=MESH)

    def remote(src, dst, send, recv, dev):
        return pltpu.make_async_remote_copy(
            src_ref=src, dst_ref=dst, send_sem=send, recv_sem=recv, device_id=dev, device_id_type=MESH
        )

    core = (z, y, other, x)

    def at_y(q):
        return (z, q, c, x)

    def at_z(q):
        return (q, y, c, x)

    def at_x(q):
        return (z, y, c, q)

    loads[0].wait()
    for r in range(0, width_in, 256):
        wkt[:, r : r + 256] = jnp.transpose(wk[r : r + 256])
    keyt[...] = jnp.zeros(keyt.shape, BF16)
    far_z = sorted(range(1, nz), key=lambda d: -min(d, nz - d))
    far_y = [d for d in (1, 3, 2) if d < ny]
    ones = jnp.ones((8, span), BF16)
    sq[...] = jnp.zeros(sq.shape, F32)

    def to_core(p):
        return remote(loc.at[p, other], r0.at[p], s0.at[p], v0.at[p], core)

    def chip_sum(p):
        to_core(p).wait_recv()
        csum[p] = (loc[p, c].astype(F32) + r0[p].astype(F32)).astype(BF16)

    def sum_to_y(p):
        return remote(csum.at[p], ry.at[y], sy.at[p], vy.at[y], at_y(p))

    def state(s, carry):
        p = turn(s)
        hid_copy(p).wait()
        kt = dot(wkt[pl.ds(pl.multiple_of(shift, 64), HL * FD)], hid[p], 1, 1).astype(BF16).astype(F32)
        live = (lax.broadcasted_iota(jnp.int32, (HL * FD, span), 1) + pos0 < len_ref[p]).astype(F32)
        kt = kt * live
        keyt[p, : HL * FD] = kt.astype(BF16)
        for h in range(HL):
            for t in range(span // 128):
                piece = kt[h * FD : (h + 1) * FD, t * 128 : (t + 1) * 128]
                kd[t, h, :FD] = piece
                kd[t, h, FD:] = piece

        @pl.when(s == 0)
        def _():
            loads[1].wait()

        val[p] = dot(hid[p], wv[...]).astype(BF16)

        @pl.when(s == 0)
        def _():
            pl.semaphore_wait(barrier, len(peers))

        @pl.when(s > 0)
        def _():
            before = turn(s - 1)
            chip_sum(before)
            sum_to_y(before).start()

        sub = lax.broadcasted_iota(jnp.int32, (8, 128), 0)
        for n in range(HL):
            pair = other if n < 2 else c
            h = pair * 2 + n % 2
            halves = []
            for t in range(span // 128):
                mine = kd[t, h, :FD]
                rows = [mine * kd[t, h, d : d + FD] for d in range(8)]
                rows += [mine[:8] * mine[8:], mine]
                rows += [jnp.where(sub == 0, live[:8, t * 128 : (t + 1) * 128], 0.0)]
                halves.append(jnp.concatenate(rows, axis=0).astype(BF16))
            feat = jnp.concatenate(halves, axis=1)
            st = dot(feat, val[p, :, pl.ds(pl.multiple_of(h * HD, HD), HD)])
            zn = dot(ones, feat, 1, 1)
            first = zn[:, :128]
            rest = jnp.concatenate([zn[:, 128:], jnp.zeros((8, 256 - ROWS), F32)], axis=1)
            tail = jnp.where(sub == 1, first, jnp.where(sub == 2, rest, st[ROWS - 8 :]))
            loc[p, pair, n % 2] = jnp.concatenate([st[: ROWS - 8], tail], axis=0).astype(BF16)
            if n == 1:
                to_core(p).start()
        return carry

    lax.fori_loop(0, ny, state, 0)

    chip_sum(y)
    ry[y] = csum[y]
    for d in range(1, ny):
        q = lax.rem(y + d, ny)
        remote(csum.at[q], ry.at[q], sy.at[q], vy.at[q], at_y(q)).wait_recv()
    total = ry[0].astype(F32)
    for q in range(1, ny):
        total = total + ry[q].astype(F32)
    total = total.reshape(2 * ROWS, HD)
    for q in range(nz):
        tz[q] = total[q * zr : (q + 1) * zr].astype(BF16)

    def slice_to_z(q):
        return remote(tz.at[q], rz.at[z], sz.at[q], vz.at[z], at_z(q))

    for d in far_z:
        slice_to_z(lax.rem(z + d, nz)).start()
    rz[z] = tz[z]

    for load in loads[2:]:
        load.wait()

    def inside(p):
        q = pltpu.roll(dot(hid[p], wq[...]), shift, 1)
        lane = lax.broadcasted_iota(jnp.int32, (span, 128), 1)
        q = jnp.where(lane < HL * FD, q, jnp.where(lane == 65, 1.0, 0.0)).astype(BF16)
        t_at = lax.broadcasted_iota(jnp.int32, (span, span), 0)
        u_at = lax.broadcasted_iota(jnp.int32, (span, span), 1)
        seen = (u_at <= t_at) & (u_at + pos0 < len_ref[p])
        row = lax.broadcasted_iota(jnp.int32, (128, span), 0)
        kt = keyt[p]
        for h in range(HL):
            phi[p, h] = (dot(q, eq[h]) * dot(q, eq[HL + h])).astype(BF16)
            mine = jnp.where((row >= h * FD) & (row < (h + 1) * FD), kt, jnp.zeros_like(kt))
            half = dot(q, mine) * 0.25 + 1.0
            weight = jnp.where(seen, half * half * 0.5 + 0.5, 0.0).astype(BF16)
            nself[p, h] = dot(weight, val[p, :, h * HD : (h + 1) * HD])
            dself[p, h] = dot(weight, jnp.ones((span, HD), BF16))

    def inside_step(p, carry):
        inside(p)
        return carry

    lax.fori_loop(0, ny // 2, inside_step, 0)

    for d in range(1, nz):
        q = lax.rem(z + d, nz)
        remote(tz.at[q], rz.at[q], sz.at[q], vz.at[q], at_z(q)).wait_recv()
    run = jnp.zeros((zr, HD), F32)
    for q in range(nz):
        pz[q] = run.astype(BF16)
        run = run + rz[q].astype(F32)
    tt[...] = run.astype(BF16)

    def prefix_to_z(q):
        return remote(pz.at[q], rpz.at[z], sz2.at[q], vz2.at[z], at_z(q))

    def total_to_z(q):
        return remote(tt, rtt.at[z], sz3.at[q], vz3.at[z], at_z(q))

    for d in far_z:
        prefix_to_z(lax.rem(z + d, nz)).start()
    rpz[z] = pz[z]
    for d in far_z:
        total_to_z(lax.rem(z + d, nz)).start()
    rtt[z] = tt[...]

    lax.fori_loop(ny // 2, ny, inside_step, 0)

    for d in range(1, nz):
        q = lax.rem(z + d, nz)
        remote(pz.at[q], rpz.at[q], sz2.at[q], vz2.at[q], at_z(q)).wait_recv()
    run = jnp.concatenate([rpz[q].astype(F32) for q in range(nz)], axis=0).reshape(2, ROWS, HD)
    for q in range(ny):
        py[q] = run.astype(BF16)
        run = run + ry[q].astype(F32)

    def prefix_to_y(q):
        return remote(py.at[q], rpy.at[y], sy2.at[q], vy2.at[y], at_y(q))

    for d in far_y:
        prefix_to_y(lax.rem(y + d, ny)).start()
    rpy[y] = py[y]

    own = sel.shape[0] // nx
    for d in range(1, nz):
        q = lax.rem(z + d, nz)
        remote(tt, rtt.at[q], sz3.at[q], vz3.at[q], at_z(q)).wait_recv()
    whole = jnp.concatenate([rtt[q].astype(F32) for q in range(nz)], axis=0).reshape(2, ROWS, HD)
    tails = jnp.concatenate([whole[0, ROWS - 8 :], whole[1, ROWS - 8 :]], axis=0).astype(BF16)
    whole = whole.astype(BF16)
    for i in range(2):
        picked = dot(sel[...], whole[i]).astype(BF16)
        for q in range(nx):
            fxs[q, i * own : (i + 1) * own] = picked[q * own : (q + 1) * own]
        lowa[y, i] = whole[i, 128:]
    for q in range(nx):
        fxs[q, 2 * own :] = tails

    def final_to_x(q):
        return remote(fxs.at[q], fxa.at[y, x], sx.at[q], vx.at[x], at_x(q))

    for d in range(1, nx):
        final_to_x(lax.rem(x + d, nx)).start()
    fxa[y, x] = fxs[x]


    def attend(p, h, state):
        tail = state[ROWS - 8 :]
        norm = jnp.concatenate(
            [jnp.broadcast_to(tail[1:2], (HD, HD)), jnp.broadcast_to(tail[2:3, : ROWS - HD], (HD, ROWS - HD))], axis=1
        ).astype(BF16)
        feats = phi[p, h]
        num = dot(feats, state.astype(BF16)) + nself[p, h]
        den = dot(feats, norm, 1, 1) + dself[p, h]
        live = lax.broadcasted_iota(jnp.int32, (span, HD), 0) + pos0 < len_ref[p]
        att[p, h] = jnp.where(live, num / den, 0.0)

    def to_core2(p):
        return remote(pc.at[p], rpc.at[p], s02.at[p], v02.at[p], core)

    at_one = (c == 1).astype(F32)

    def near(p):
        chip = rpy[p].astype(F32)
        pc[p] = (chip + (1.0 - at_one) * loc[p, c].astype(F32)).astype(BF16)
        to_core2(p).start()
        mine = chip + at_one * r0[p].astype(F32)
        for i in range(2):
            attend(p, c * 2 + i, mine[i])

    def far(p):
        to_core2(p).wait_recv()
        there = rpc[p].astype(F32)
        for i in range(2):
            attend(p, other * 2 + i, there[i])
        square = att[p, 0] * att[p, 0]
        for h in range(1, HL):
            square = square + att[p, h] * att[p, h]
        high = square.astype(BF16)
        rest = (square - high.astype(F32)).astype(BF16)
        unit = jnp.ones((8, HD), BF16)
        sq[pl.ds(p, 1)] = (dot(unit, high, 1, 1) + dot(unit, rest, 1, 1))[0:1]

    def final_to_core(p):
        return remote(fxa.at[p], fx_hbm.at[c, p], s3.at[p], v3.at[p], core)

    def low_to_core(p):
        return remote(lowa.at[p], low_hbm.at[c, p], s4.at[p], v4.at[p], core)

    def final_here(p):
        return pltpu.make_async_copy(fxa.at[p], fx_hbm.at[c, p], osem.at[ny + p])

    def low_here(p):
        return pltpu.make_async_copy(lowa.at[p], low_hbm.at[c, p], osem.at[2 * ny + p])

    def deliver(p):
        for copy in (final_to_core(p), low_to_core(p), final_here(p), low_here(p)):
            copy.start()

    def turn_back(s):
        return lax.rem(y + jnp.where(s == 0, 3, s), ny)

    def near_step(s, carry):
        p = turn_back(s)
        remote(py.at[p], rpy.at[p], sy2.at[p], vy2.at[p], at_y(p)).wait_recv()
        near(p)
        return carry

    def far_step(s, carry):
        far(turn_back(s))
        return carry

    near(y)
    lax.fori_loop(0, ny - 1, near_step, 0)
    far(y)

    for d in range(1, nx):
        q = lax.rem(x + d, nx)
        remote(fxs.at[q], fxa.at[y, q], sx.at[q], vx.at[q], at_x(q)).wait_recv()

    def final_to_y(q):
        return remote(fxa.at[y], fxa.at[y], sy3.at[q], vy3.at[y], at_y(q))

    def low_to_y(q):
        return remote(lowa.at[y], lowa.at[y], sy4.at[q], vy4.at[y], at_y(q))

    for d in far_y:
        q = lax.rem(y + d, ny)
        final_to_y(q).start()
        low_to_y(q).start()

    deliver(y)
    lax.fori_loop(0, ny - 1, far_step, 0)

    def square_to_x(q):
        return remote(sq, rsq.at[x], sx2.at[q], vx2.at[x], at_x(q))

    for d in range(1, nx):
        square_to_x(lax.rem(x + d, nx)).start()

    rsq[x] = sq[...]
    for d in range(1, nx):
        q = lax.rem(x + d, nx)
        remote(sq, rsq.at[q], sx2.at[q], vx2.at[q], at_x(q)).wait_recv()

    def mixed_out(p):
        return pltpu.make_async_copy(mixed.at[p], mixed_hbm.at[p], osem.at[p])

    squares = rsq[0]
    for q in range(1, nx):
        squares = squares + rsq[q]
    factor = jnp.transpose(lax.rsqrt(squares / width + NORM_FLOOR))
    for p in range(ny):
        scale = jnp.broadcast_to(factor[:, p : p + 1], (span, HD))
        for h in range(HL):
            mixed[p, :, h * HD : (h + 1) * HD] = (att[p, h] * scale).astype(BF16)
        mixed_out(p).start()

    for s in (3, 1, 2):
        q = lax.rem(y + s, ny)
        remote(fxa.at[y], fxa.at[q], sy3.at[q], vy3.at[q], at_y(q)).wait_recv()
        remote(lowa.at[y], lowa.at[q], sy4.at[q], vy4.at[q], at_y(q)).wait_recv()
        deliver(q)

    for p in range(ny):
        remote(fxa.at[p], fx_hbm.at[other, p], s3.at[p], v3.at[p], core).wait_recv()
        remote(lowa.at[p], low_hbm.at[other, p], s4.at[p], v4.at[p], core).wait_recv()

    for p in range(ny):
        to_core(p).wait_send()
        to_core2(p).wait_send()
    for d in range(1, ny):
        q = lax.rem(y + d, ny)
        sum_to_y(q).wait_send()
        prefix_to_y(q).wait_send()
        final_to_y(q).wait_send()
        low_to_y(q).wait_send()
    for d in range(1, nz):
        q = lax.rem(z + d, nz)
        slice_to_z(q).wait_send()
        prefix_to_z(q).wait_send()
        total_to_z(q).wait_send()
    for d in range(1, nx):
        q = lax.rem(x + d, nx)
        final_to_x(q).wait_send()
        square_to_x(q).wait_send()
    for p in range(ny):
        final_to_core(p).wait_send()
        low_to_core(p).wait_send()
        final_here(p).wait()
        low_here(p).wait()
        mixed_out(p).wait()


def finish(
    sizes, own_ref, scaled_hbm, fx_hbm, low_hbm, sel_hbm, mixed_hbm, quad_hbm, slow_hbm, nquad_hbm, nlow_hbm,
    fx, low, sel, mixed, quad, slow, nquad, nlow, isem, osem,
):
    nz, ny, nc, nx, prompts = sizes
    z, y, c, x = (lax.axis_index(a) for a in ("z", "y", "c", "x"))
    here = (z * ny + y) * nc + c
    own = sel.shape[0]

    def mixed_in(p):
        return pltpu.make_async_copy(scaled_hbm.at[p], mixed.at[p], isem.at[p])

    def fx_in(p):
        return pltpu.make_async_copy(fx_hbm.at[:, p], fx.at[:, p], isem.at[prompts + p])

    def out_copies(p):
        return [
            pltpu.make_async_copy(quad.at[p], quad_hbm.at[0, p], osem.at[prompts + p]),
            pltpu.make_async_copy(slow.at[p], slow_hbm.at[0, p], osem.at[2 * prompts + p]),
            pltpu.make_async_copy(nquad.at[p], nquad_hbm.at[0, p], osem.at[3 * prompts + p]),
            pltpu.make_async_copy(nlow.at[p], nlow_hbm.at[0, p], osem.at[4 * prompts + p]),
        ]

    def mixed_out(p):
        return pltpu.make_async_copy(mixed.at[p], mixed_hbm.at[p], osem.at[p])

    small = [
        pltpu.make_async_copy(low_hbm, low, isem.at[2 * prompts]),
        pltpu.make_async_copy(sel_hbm.at[pl.ds(pl.multiple_of(x * own, own), own)], sel, isem.at[2 * prompts + 1]),
    ]
    for p in range(prompts):
        mixed_in(p).start()
    small[0].start()
    small[1].start()
    for p in range(prompts):

        @pl.when(own_ref[p] == here)
        def _():
            fx_in(p).start()

        @pl.when(own_ref[p] != here)
        def _():
            quad[p] = jnp.zeros(quad.shape[1:], F32)
            slow[p] = jnp.zeros(slow.shape[1:], F32)
            nquad[p] = jnp.zeros(nquad.shape[1:], F32)
            nlow[p] = jnp.zeros(nlow.shape[1:], F32)
            for copy in out_copies(p):
                copy.start()

    for p in range(prompts):
        mixed_in(p).wait()
        mixed_out(p).start()

    small[0].wait()
    small[1].wait()
    quad_scale = (2.0 * FD) ** (-0.5)
    low_scale = FD ** (-0.25)
    lin, one = LIN - 128, ONE - 128
    for p in range(prompts):

        @pl.when(own_ref[p] == here)
        def _():
            fx_in(p).wait()
            first, rest = [], []
            for g in range(nx):
                for k in range(nc):
                    block = fx[k, p, g].astype(F32)
                    for i in range(2):
                        quad[p, g * HL + k * 2 + i] = block[i * own : (i + 1) * own] * quad_scale
                        at = 2 * own + i * 8 + NORM - (ROWS - 8)
                        first.append(block[at : at + 1])
                        rest.append(block[at + 1 : at + 2, : ROWS - 128])
            norms = jnp.concatenate([jnp.concatenate(first, axis=0), jnp.concatenate(rest, axis=0)], axis=1)
            nquad[p] = dot(norms.astype(BF16), sel[...], 1, 1) * quad_scale
            for k in range(nc):
                for i in range(2):
                    rows = low[k, p, i].astype(F32)
                    slow[p, 0, pl.ds(k * 2 + i, 1)] = rows[one : one + 1]
                    for r in range(FD):
                        slow[p, 1 + r, pl.ds(k * 2 + i, 1)] = rows[lin + r : lin + r + 1] * low_scale
                    tail = rows[NORM + 1 - 128 : NORM + 2 - 128]
                    nlow[p, pl.ds(k * 2 + i, 1)] = jnp.concatenate(
                        [tail[:, one : one + 1], tail[:, lin : lin + FD] * low_scale], axis=1
                    )
            for copy in out_copies(p):
                copy.start()

    for p in range(prompts):
        mixed_out(p).wait()
        for copy in out_copies(p):
            copy.wait()


def body(hidden_in, w_query, w_key, w_value, lengths, owners):
    nz, ny, nc, nx = (lax.axis_size(a) for a in ("z", "y", "c", "x"))
    prompts, span, width = hidden_in.shape
    own = FD // nx * FD
    part = 2 * own + 16
    zr = 2 * ROWS // nz
    wide = HD * HL * nx
    eq, sel = (jnp.asarray(t) for t in tables(nx))
    anyspace = pl.BlockSpec(memory_space=pl.ANY)
    scalars = pl.BlockSpec(memory_space=pltpu.SMEM)
    dma = pltpu.SemaphoreType.DMA

    def vmem(*shape, kind=BF16):
        return pltpu.VMEM(shape, kind)

    def array(*shape, kind=F32):
        return jax.ShapeDtypeStruct(shape, kind)

    block = (2, ROWS, HD)
    scaled, fx, low = pl.pallas_call(
        functools.partial(kernel, (nz, ny, nc, nx, span, wide)),
        out_shape=(
            array(prompts, span, HL * HD, kind=BF16),
            array(nc, prompts, nx, part, HD, kind=BF16),
            array(nc, prompts, 2, ROWS - 128, HD, kind=BF16),
        ),
        in_specs=[scalars] + [anyspace] * 6,
        out_specs=(anyspace,) * 3,
        scratch_shapes=[
            vmem(prompts, span, width), vmem(width, HL * HD), vmem(width, 128), vmem(128, width), vmem(width, 128),
            vmem(*eq.shape), vmem(*sel.shape),
            vmem(prompts, span, HL * HD), vmem(prompts, 128, span), vmem(span // 128, HL, 2 * FD, 128, kind=F32),
            vmem(prompts, HL, span, ROWS),
            vmem(prompts, HL, span, HD, kind=F32), vmem(prompts, HL, span, HD, kind=F32),
            vmem(prompts, HL, span, HD, kind=F32),
            vmem(prompts, span, HL * HD), vmem(8, span, kind=F32), vmem(nx, 8, span, kind=F32),
            vmem(prompts, 2, *block), vmem(prompts, *block), vmem(prompts, *block), vmem(ny, *block),
            vmem(nz, zr, HD), vmem(nz, zr, HD), vmem(nz, zr, HD), vmem(nz, zr, HD), vmem(zr, HD), vmem(nz, zr, HD),
            vmem(ny, *block), vmem(prompts, *block), vmem(prompts, *block), vmem(prompts, *block),
            vmem(nx, part, HD), vmem(prompts, nx, part, HD), vmem(prompts, 2, ROWS - 128, HD),
            dma((5,)), dma((prompts,)), dma((prompts,)), dma((prompts,)),
            dma((ny,)), dma((ny,)), dma((nz,)), dma((nz,)), dma((nz,)), dma((nz,)), dma((nz,)), dma((nz,)),
            dma((ny,)), dma((ny,)), dma((prompts,)), dma((prompts,)),
            dma((nx,)), dma((nx,)), dma((ny,)), dma((ny,)), dma((ny,)), dma((ny,)),
            dma((ny,)), dma((ny,)), dma((ny,)), dma((ny,)),
            dma((nx,)), dma((nx,)), dma((3 * prompts + 1,)),
        ],
        compiler_params=pltpu.CompilerParams(
            collective_id=0, has_side_effects=True, vmem_limit_bytes=60 * 1024 * 1024
        ),
        name="prefill",
    )(lengths, hidden_in, w_value, w_key, w_query, eq, sel)

    mixed, quad, state_low, nquad, nlow = pl.pallas_call(
        functools.partial(finish, (nz, ny, nc, nx, prompts)),
        out_shape=(
            array(prompts, span, HL * HD, kind=BF16),
            array(1, prompts, HL * nx, own, HD),
            array(1, prompts, FD + 1, HL, HD),
            array(1, prompts, HL * nx, own),
            array(1, prompts, HL, FD + 1),
        ),
        in_specs=[scalars] + [anyspace] * 4,
        out_specs=(anyspace,) * 5,
        scratch_shapes=[
            vmem(nc, prompts, nx, part, HD),
            vmem(nc, prompts, 2, ROWS - 128, HD), vmem(own, ROWS), vmem(prompts, span, HL * HD),
            vmem(prompts, HL * nx, own, HD, kind=F32), vmem(prompts, FD + 1, HL, HD, kind=F32),
            vmem(prompts, HL * nx, own, kind=F32), vmem(prompts, HL, FD + 1, kind=F32),
            dma((2 * prompts + 2,)), dma((5 * prompts,)),
        ],
        compiler_params=pltpu.CompilerParams(vmem_limit_bytes=60 * 1024 * 1024),
        name="finish",
    )(owners, scaled, fx, low, sel)
    return mixed, quad, jnp.transpose(state_low, (0, 1, 3, 2, 4)), nquad, nlow


def torus_of(mesh, shape=(8, 4, 2, 4)):
    return Mesh(mesh.devices.reshape(shape), ("z", "y", "c", "x"))


def run_on(torus):
    return jax.shard_map(
        body,
        mesh=torus,
        in_specs=(P(None, SEQ, None), P(), P(), P(None, "x"), P(), P()),
        out_specs=(
            P(None, SEQ, "x"),
            P(SEQ, None, None, "x", None),
            P(SEQ, None, "x", None, None),
            P(SEQ, None, None, "x"),
            P(SEQ, None, "x", None),
        ),
        check_vma=False,
    )


def solution(mesh):
    ny, nc = 4, 2
    feat = mesh.shape["feat"]
    return run_on(torus_of(mesh, (mesh.shape["seq"] // (ny * nc), ny, nc, feat)))
```

time: 59.6 us -> 49.4 us (0.83)
  local copies, waits for them, and re-layouts: 3.3 us -> 0 us
  other arithmetic: 3.24 us -> 0 us
  Pallas kernels: 50.6 us -> 48.6 us
  matrix products: 1.52 us -> 0 us
    pallas_call x1 -> x2, Pallas kernels: 50.6 us -> 48.6 us  [the longest x1 45.2 us: body(): pl.pallas_call(functools.partial(kernel, (nz, ny, nc, nx, span, wide)), o...]
    broadcast_in_dim x1 -> x0, other arithmetic: 1.71 us -> none  [body(): jnp.where(owned[:, None, None, None], fx[:, :, :own].astype(F32) * quad_s...]
    unnamed x8 -> x0, local copies, waits for them, and re-layouts: 1.68 us -> none
    dot_general x1 -> x0, matrix products: 1.52 us -> none  [dot(): lax.dot_general(a, b, (((ca,), (cb,)), ((), ())), preferred_element_type=...]
    transpose x2 -> x0, local copies, waits for them, and re-layouts: 1.49 us -> none  [the longest x1 1.48 us: body(): jnp.transpose(fx, (1, 2, 0, 3, 4, 5)).reshape(prompts, HL * nx, part, HD)]
    select_n x2 -> x0, other arithmetic: 0.77 us -> none  [the longest x1 0.68 us: body(): norm_low = jnp.where(owned[:, None, None], norm_low, 0.0)[None]]
    eq x1 -> x0, other arithmetic: 0.66 us -> none  [body(): owned = owners == lax.axis_index(SEQ)]
where the time goes in v2:
time: 49.4 us; the launch traced here: 49.3 us
  Pallas kernels  48.6 us (98%)
  between operations  0.64 us (1%)
    pallas_call x1, Pallas kernels, body(): pl.pallas_call(functools.partial(kernel, (nz, ny, nc, nx, span, wide)), o...  45.2 us
    pallas_call x1, Pallas kernels, body(): pl.pallas_call(functools.partial(finish, (nz, ny, nc, nx, prompts)), out_...  3.42 us

profile of v2, /device:TPU:1, one launch (start us, length us, event | category | flops | bytes accessed | tf_op | source)
XLA Modules:
  0.0 49.3 jit_solution(6885869419248050915)
XLA Ops:
  0.6 45.2 %prefill.1 = (bf16[4,256,512]{2,1,0:T(8,128)(2,1)}, bf16[2,4,4,144,128]{4,3,2,1,0:T(8,128)(2,1)}, bf16[2,4,2,32,128]{4,3,2,1,0:T(8,128)(2,1)}) custom-call(s32[4]{0:T(128)} %len_ref.1, bf16[4,256,2048]{2,1,0:T(8,128)(2,1)} %hid_hbm.1, bf16[2048,512]{1,0:T(8,128)(2,1)} %wv_hbm.1, bf16[2048,256]{1,0:T(8,128)(2,1)} %wk_hbm.1, bf16[2048,256]{1,0:T(8,128)(2,1)} %wq_hbm.1, ...), custom_call_target="tpu_custom_call" | custom-call | tf_op jit(solution)/shard_map/prefill/pallas_call | solution.py:565
  45.9 3.4 %finish.1 = (bf16[4,256,512]{2,1,0:T(8,128)(2,1)}, f32[1,4,16,64,128]{4,3,2,1,0:T(8,128)}, f32[1,4,17,4,128]{4,3,2,1,0:T(4,128)}, f32[1,4,16,64]{3,2,1,0:T(8,128)}, f32[1,4,4,17]{3,2,1,0:T(4,128)}) custom-call(s32[4]{0:T(128)} %own_ref.1, bf16[4,256,512]{2,1,0:T(8,128)(2,1)} %get-tuple-element.13.scaled_hbm, ...), custom_call_target="tpu_custom_call" | custom-call | tf_op jit(solution)/shard_map/finish/pallas_call | solution.py:599

commit v3 on v2

--- a/solution.py
+++ b/solution.py
@@ -18,6 +18,7 @@
 NORM_FLOOR = 0.0001
 HL = 4
 SEQ = ("z", "y", "c")
+LIMIT1, LIMIT2 = 44 << 20, 16 << 20
 
 
 def packed_pairs():
@@ -62,9 +63,9 @@
 
 
 def kernel(
-    sizes, len_ref, hid_hbm, wv_hbm, wk_hbm, wq_hbm, eq_hbm, sel_hbm, mixed_hbm, fx_hbm, low_hbm,
-    hid, wv, wk, wkt, wq, eq, sel, val, keyt, kd, phi, nself, dself, att, mixed, sq, rsq,
-    loc, r0, csum, ry, tz, rz, pz, rpz, tt, rtt, py, rpy, pc, rpc, fxs, fxa, lowa,
+    sizes, len_ref, hid_hbm, wv_hbm, wk_hbm, wq_hbm, eq_hbm, sel_hbm, mixed, fx_all, low_all,
+    hid, wv, wk, wkt, wq, eq, sel, val, keyt, kd, phi, nself, dself, att, sq, rsq,
+    loc, r0, csum, ry, cut, whole_total, rz, pz, rpz, tt, rtt, py, rpy, pc, rpc, fxs, fxa, lowa,
     lsem, hsem, s0, v0, sy, vy, sz, vz, sz2, vz2, sz3, vz3, sy2, vy2, s02, v02,
     sx, vx, sy3, vy3, sy4, vy4, s3, v3, s4, v4, sx2, vx2, osem,
 ):
@@ -81,22 +82,41 @@
     def turn(s):
         return lax.rem(y + jnp.where(s == 0, 2, jnp.where(s == 1, 1, jnp.where(s == 2, 3, 0))), ny)
 
-    def hid_copy(p):
-        return pltpu.make_async_copy(hid_hbm.at[p], hid.at[p], hsem.at[p])
-
+    def hid_copies(p):
+        rows = span // 4
+        return [
+            pltpu.make_async_copy(hid_hbm.at[p, pl.ds(i * rows, rows)], hid.at[p, pl.ds(i * rows, rows)], hsem.at[p, i])
+            for i in range(4)
+        ]
+
+    def start_hid(p):
+        for copy in hid_copies(p):
+            copy.start()
+
+    deep = width_in // 4
+    wk_loads = [
+        pltpu.make_async_copy(
+            wk_hbm.at[pl.ds(i * deep, deep), pl.ds(col, 128)], wk.at[pl.ds(i * deep, deep)], lsem.at[i]
+        )
+        for i in range(4)
+    ]
+    wv_loads = [
+        pltpu.make_async_copy(wv_hbm.at[pl.ds(i * deep, deep)], wv.at[pl.ds(i * deep, deep)], lsem.at[4 + i])
+        for i in range(4)
+    ]
     loads = [
-        pltpu.make_async_copy(wk_hbm.at[:, pl.ds(col, 128)], wk, lsem.at[0]),
-        pltpu.make_async_copy(wv_hbm, wv, lsem.at[1]),
-        pltpu.make_async_copy(wq_hbm.at[:, pl.ds(col, 128)], wq, lsem.at[2]),
-        pltpu.make_async_copy(eq_hbm, eq, lsem.at[3]),
-        pltpu.make_async_copy(sel_hbm, sel, lsem.at[4]),
+        pltpu.make_async_copy(wq_hbm.at[:, pl.ds(col, 128)], wq, lsem.at[8]),
+        pltpu.make_async_copy(eq_hbm, eq, lsem.at[9]),
+        pltpu.make_async_copy(sel_hbm, sel, lsem.at[10]),
     ]
-    loads[0].start()
-    hid_copy(turn(0)).start()
-    loads[1].start()
+    for load in wk_loads:
+        load.start()
+    start_hid(turn(0))
+    for load in wv_loads:
+        load.start()
     for s in range(1, ny):
-        hid_copy(turn(s)).start()
-    for load in loads[2:]:
+        start_hid(turn(s))
+    for load in loads:
         load.start()
 
     barrier = pltpu.get_barrier_semaphore()
@@ -123,9 +143,9 @@
     def at_x(q):
         return (z, y, c, q)
 
-    loads[0].wait()
-    for r in range(0, width_in, 256):
-        wkt[:, r : r + 256] = jnp.transpose(wk[r : r + 256])
+    for i in range(4):
+        wk_loads[i].wait()
+        wkt[:, i * deep : (i + 1) * deep] = jnp.transpose(wk[i * deep : (i + 1) * deep])
     keyt[...] = jnp.zeros(keyt.shape, BF16)
     far_z = sorted(range(1, nz), key=lambda d: -min(d, nz - d))
     far_y = [d for d in (1, 3, 2) if d < ny]
@@ -135,19 +155,25 @@
     def to_core(p):
         return remote(loc.at[p, other], r0.at[p], s0.at[p], v0.at[p], core)
 
-    def chip_sum(p):
-        to_core(p).wait_recv()
-        csum[p] = (loc[p, c].astype(F32) + r0[p].astype(F32)).astype(BF16)
-
     def sum_to_y(p):
         return remote(csum.at[p], ry.at[y], sy.at[p], vy.at[y], at_y(p))
 
-    def state(s, carry):
+    def slice_to(q):
+        return remote(cut.at[q], rz.at[z], sz.at[q], vz.at[z], at_z(q))
+
+    def chip(p, own):
+        to_core(p).wait_recv()
+        both = loc[p, c].astype(F32) + r0[p].astype(F32)
+        csum[p] = both.astype(BF16)
+        if not own:
+            sum_to_y(p).start()
+
+    def keys(s):
         p = turn(s)
-        hid_copy(p).wait()
+        for copy in hid_copies(p):
+            copy.wait()
         kt = dot(wkt[pl.ds(pl.multiple_of(shift, 64), HL * FD)], hid[p], 1, 1).astype(BF16).astype(F32)
-        live = (lax.broadcasted_iota(jnp.int32, (HL * FD, span), 1) + pos0 < len_ref[p]).astype(F32)
-        kt = kt * live
+        kt = kt * (lax.broadcasted_iota(jnp.int32, (HL * FD, span), 1) + pos0 < len_ref[p]).astype(F32)
         keyt[p, : HL * FD] = kt.astype(BF16)
         for h in range(HL):
             for t in range(span // 128):
@@ -155,22 +181,12 @@
                 kd[t, h, :FD] = piece
                 kd[t, h, FD:] = piece
 
-        @pl.when(s == 0)
-        def _():
-            loads[1].wait()
-
+    def values(s):
+        p = turn(s)
         val[p] = dot(hid[p], wv[...]).astype(BF16)
 
-        @pl.when(s == 0)
-        def _():
-            pl.semaphore_wait(barrier, len(peers))
-
-        @pl.when(s > 0)
-        def _():
-            before = turn(s - 1)
-            chip_sum(before)
-            sum_to_y(before).start()
-
+    def state(s):
+        p = turn(s)
         sub = lax.broadcasted_iota(jnp.int32, (8, 128), 0)
         for n in range(HL):
             pair = other if n < 2 else c
@@ -178,9 +194,10 @@
             halves = []
             for t in range(span // 128):
                 mine = kd[t, h, :FD]
+                at = lax.broadcasted_iota(jnp.int32, (8, 128), 1) + (pos0 + t * 128)
                 rows = [mine * kd[t, h, d : d + FD] for d in range(8)]
                 rows += [mine[:8] * mine[8:], mine]
-                rows += [jnp.where(sub == 0, live[:8, t * 128 : (t + 1) * 128], 0.0)]
+                rows += [jnp.where((sub == 0) & (at < len_ref[p]), 1.0, 0.0)]
                 halves.append(jnp.concatenate(rows, axis=0).astype(BF16))
             feat = jnp.concatenate(halves, axis=1)
             st = dot(feat, val[p, :, pl.ds(pl.multiple_of(h * HD, HD), HD)])
@@ -191,11 +208,32 @@
             loc[p, pair, n % 2] = jnp.concatenate([st[: ROWS - 8], tail], axis=0).astype(BF16)
             if n == 1:
                 to_core(p).start()
+
+    keys(0)
+    for load in wv_loads:
+        load.wait()
+    values(0)
+    pl.semaphore_wait(barrier, len(peers))
+
+    def step(s, carry):
+        state(s)
+        keys(s + 1)
+
+        @pl.when(s == ny - 2)
+        def _():
+            chip(turn(s), False)
+
+        values(s + 1)
+
+        @pl.when(s < ny - 2)
+        def _():
+            chip(turn(s), False)
+
         return carry
 
-    lax.fori_loop(0, ny, state, 0)
-
-    chip_sum(y)
+    lax.fori_loop(0, ny - 1, step, 0)
+    state(ny - 1)
+    chip(y, True)
     ry[y] = csum[y]
     for d in range(1, ny):
         q = lax.rem(y + d, ny)
@@ -203,18 +241,14 @@
     total = ry[0].astype(F32)
     for q in range(1, ny):
         total = total + ry[q].astype(F32)
-    total = total.reshape(2 * ROWS, HD)
+    whole_total[...] = total.reshape(2 * ROWS, HD)
+    flat = whole_total[...]
     for q in range(nz):
-        tz[q] = total[q * zr : (q + 1) * zr].astype(BF16)
-
-    def slice_to_z(q):
-        return remote(tz.at[q], rz.at[z], sz.at[q], vz.at[z], at_z(q))
-
+        cut[q] = flat[q * zr : (q + 1) * zr].astype(BF16)
     for d in far_z:
-        slice_to_z(lax.rem(z + d, nz)).start()
-    rz[z] = tz[z]
-
-    for load in loads[2:]:
+        slice_to(lax.rem(z + d, nz)).start()
+    rz[z] = cut[z]
+    for load in loads:
         load.wait()
 
     def inside(p):
@@ -242,7 +276,7 @@
 
     for d in range(1, nz):
         q = lax.rem(z + d, nz)
-        remote(tz.at[q], rz.at[q], sz.at[q], vz.at[q], at_z(q)).wait_recv()
+        remote(cut.at[q], rz.at[q], sz.at[q], vz.at[q], at_z(q)).wait_recv()
     run = jnp.zeros((zr, HD), F32)
     for q in range(nz):
         pz[q] = run.astype(BF16)
@@ -340,37 +374,34 @@
         sq[pl.ds(p, 1)] = (dot(unit, high, 1, 1) + dot(unit, rest, 1, 1))[0:1]
 
     def final_to_core(p):
-        return remote(fxa.at[p], fx_hbm.at[c, p], s3.at[p], v3.at[p], core)
+        return remote(fxa.at[p], fx_all.at[c, p], s3.at[p], v3.at[p], core)
 
     def low_to_core(p):
-        return remote(lowa.at[p], low_hbm.at[c, p], s4.at[p], v4.at[p], core)
+        return remote(lowa.at[p], low_all.at[c, p], s4.at[p], v4.at[p], core)
 
     def final_here(p):
-        return pltpu.make_async_copy(fxa.at[p], fx_hbm.at[c, p], osem.at[ny + p])
+        return pltpu.make_async_copy(fxa.at[p], fx_all.at[c, p], osem.at[p])
 
     def low_here(p):
-        return pltpu.make_async_copy(lowa.at[p], low_hbm.at[c, p], osem.at[2 * ny + p])
+        return pltpu.make_async_copy(lowa.at[p], low_all.at[c, p], osem.at[ny + p])
 
     def deliver(p):
         for copy in (final_to_core(p), low_to_core(p), final_here(p), low_here(p)):
             copy.start()
 
-    def turn_back(s):
-        return lax.rem(y + jnp.where(s == 0, 3, s), ny)
-
-    def near_step(s, carry):
-        p = turn_back(s)
+    def arrived(d):
+        p = lax.rem(y + d, ny)
         remote(py.at[p], rpy.at[p], sy2.at[p], vy2.at[p], at_y(p)).wait_recv()
-        near(p)
-        return carry
-
-    def far_step(s, carry):
-        far(turn_back(s))
-        return carry
+        return p
 
     near(y)
-    lax.fori_loop(0, ny - 1, near_step, 0)
-    far(y)
+
+    @pl.when(c == 0)
+    def _():
+        far(y)
+
+    near(arrived(3))
+    near(arrived(1))
 
     for d in range(1, nx):
         q = lax.rem(x + d, nx)
@@ -388,7 +419,15 @@
         low_to_y(q).start()
 
     deliver(y)
-    lax.fori_loop(0, ny - 1, far_step, 0)
+
+    @pl.when(c == 1)
+    def _():
+        far(y)
+
+    far(lax.rem(y + 3, ny))
+    near(arrived(2))
+    far(lax.rem(y + 1, ny))
+    far(lax.rem(y + 2, ny))
 
     def square_to_x(q):
         return remote(sq, rsq.at[x], sx2.at[q], vx2.at[x], at_x(q))
@@ -400,9 +439,6 @@
     for d in range(1, nx):
         q = lax.rem(x + d, nx)
         remote(sq, rsq.at[q], sx2.at[q], vx2.at[q], at_x(q)).wait_recv()
-
-    def mixed_out(p):
-        return pltpu.make_async_copy(mixed.at[p], mixed_hbm.at[p], osem.at[p])
 
     squares = rsq[0]
     for q in range(1, nx):
@@ -412,7 +448,6 @@
         scale = jnp.broadcast_to(factor[:, p : p + 1], (span, HD))
         for h in range(HL):
             mixed[p, :, h * HD : (h + 1) * HD] = (att[p, h] * scale).astype(BF16)
-        mixed_out(p).start()
 
     for s in (3, 1, 2):
         q = lax.rem(y + s, ny)
@@ -421,8 +456,8 @@
         deliver(q)
 
     for p in range(ny):
-        remote(fxa.at[p], fx_hbm.at[other, p], s3.at[p], v3.at[p], core).wait_recv()
-        remote(lowa.at[p], low_hbm.at[other, p], s4.at[p], v4.at[p], core).wait_recv()
+        remote(fxa.at[p], fx_all.at[other, p], s3.at[p], v3.at[p], core).wait_recv()
+        remote(lowa.at[p], low_all.at[other, p], s4.at[p], v4.at[p], core).wait_recv()
 
     for p in range(ny):
         to_core(p).wait_send()
@@ -435,7 +470,7 @@
         low_to_y(q).wait_send()
     for d in range(1, nz):
         q = lax.rem(z + d, nz)
-        slice_to_z(q).wait_send()
+        slice_to(q).wait_send()
         prefix_to_z(q).wait_send()
         total_to_z(q).wait_send()
     for d in range(1, nx):
@@ -447,27 +482,20 @@
         low_to_core(p).wait_send()
         final_here(p).wait()
         low_here(p).wait()
-        mixed_out(p).wait()
 
 
 def finish(
-    sizes, own_ref, scaled_hbm, fx_hbm, low_hbm, sel_hbm, mixed_hbm, quad_hbm, slow_hbm, nquad_hbm, nlow_hbm,
-    fx, low, sel, mixed, quad, slow, nquad, nlow, isem, osem,
+    sizes, own_ref, mixed, fx, low, sel_hbm, mixed_hbm, quad_hbm, slow_hbm, nquad_hbm, nlow_hbm,
+    sel, quad, slow, nquad, nlow, isem, osem,
 ):
     nz, ny, nc, nx, prompts = sizes
     z, y, c, x = (lax.axis_index(a) for a in ("z", "y", "c", "x"))
     here = (z * ny + y) * nc + c
     own = sel.shape[0]
 
-    def mixed_in(p):
-        return pltpu.make_async_copy(scaled_hbm.at[p], mixed.at[p], isem.at[p])
-
-    def fx_in(p):
-        return pltpu.make_async_copy(fx_hbm.at[:, p], fx.at[:, p], isem.at[prompts + p])
-
-    def out_copies(p):
+    def out_copies(p, at):
         return [
-            pltpu.make_async_copy(quad.at[p], quad_hbm.at[0, p], osem.at[prompts + p]),
+            pltpu.make_async_copy(quad.at[at], quad_hbm.at[0, p], osem.at[prompts + p]),
             pltpu.make_async_copy(slow.at[p], slow_hbm.at[0, p], osem.at[2 * prompts + p]),
             pltpu.make_async_copy(nquad.at[p], nquad_hbm.at[0, p], osem.at[3 * prompts + p]),
             pltpu.make_async_copy(nlow.at[p], nlow_hbm.at[0, p], osem.at[4 * prompts + p]),
@@ -476,35 +504,22 @@
     def mixed_out(p):
         return pltpu.make_async_copy(mixed.at[p], mixed_hbm.at[p], osem.at[p])
 
-    small = [
-        pltpu.make_async_copy(low_hbm, low, isem.at[2 * prompts]),
-        pltpu.make_async_copy(sel_hbm.at[pl.ds(pl.multiple_of(x * own, own), own)], sel, isem.at[2 * prompts + 1]),
-    ]
+    sel_in = pltpu.make_async_copy(sel_hbm.at[pl.ds(pl.multiple_of(x * own, own), own)], sel, isem.at[0])
+    sel_in.start()
     for p in range(prompts):
-        mixed_in(p).start()
-    small[0].start()
-    small[1].start()
+        mixed_out(p).start()
+    quad[prompts] = jnp.zeros(quad.shape[1:], F32)
+    slow[...] = jnp.zeros(slow.shape, F32)
+    nquad[...] = jnp.zeros(nquad.shape, F32)
+    nlow[...] = jnp.zeros(nlow.shape, F32)
     for p in range(prompts):
-
-        @pl.when(own_ref[p] == here)
-        def _():
-            fx_in(p).start()
 
         @pl.when(own_ref[p] != here)
         def _():
-            quad[p] = jnp.zeros(quad.shape[1:], F32)
-            slow[p] = jnp.zeros(slow.shape[1:], F32)
-            nquad[p] = jnp.zeros(nquad.shape[1:], F32)
-            nlow[p] = jnp.zeros(nlow.shape[1:], F32)
-            for copy in out_copies(p):
+            for copy in out_copies(p, prompts):
                 copy.start()
 
-    for p in range(prompts):
-        mixed_in(p).wait()
-        mixed_out(p).start()
-
-    small[0].wait()
-    small[1].wait()
+    sel_in.wait()
     quad_scale = (2.0 * FD) ** (-0.5)
     low_scale = FD ** (-0.25)
     lin, one = LIN - 128, ONE - 128
@@ -512,7 +527,6 @@
 
         @pl.when(own_ref[p] == here)
         def _():
-            fx_in(p).wait()
             first, rest = [], []
             for g in range(nx):
                 for k in range(nc):
@@ -534,12 +548,12 @@
                     nlow[p, pl.ds(k * 2 + i, 1)] = jnp.concatenate(
                         [tail[:, one : one + 1], tail[:, lin : lin + FD] * low_scale], axis=1
                     )
-            for copy in out_copies(p):
+            for copy in out_copies(p, p):
                 copy.start()
 
     for p in range(prompts):
         mixed_out(p).wait()
-        for copy in out_copies(p):
+        for copy in out_copies(p, p):
             copy.wait()
 
 
@@ -551,7 +565,12 @@
     zr = 2 * ROWS // nz
     wide = HD * HL * nx
     eq, sel = (jnp.asarray(t) for t in tables(nx))
-    anyspace = pl.BlockSpec(memory_space=pl.ANY)
+    lengths, owners, hidden_in, w_value, w_key, w_query, eq, sel = (
+        pltpu.with_memory_space_constraint(a, pltpu.HBM)
+        for a in (lengths, owners, hidden_in, w_value, w_key, w_query, eq, sel)
+    )
+    hbm = pl.BlockSpec(memory_space=pltpu.HBM)
+    whole = pl.BlockSpec(memory_space=pltpu.VMEM)
     scalars = pl.BlockSpec(memory_space=pltpu.SMEM)
     dma = pltpu.SemaphoreType.DMA
 
@@ -569,8 +588,8 @@
             array(nc, prompts, nx, part, HD, kind=BF16),
             array(nc, prompts, 2, ROWS - 128, HD, kind=BF16),
         ),
-        in_specs=[scalars] + [anyspace] * 6,
-        out_specs=(anyspace,) * 3,
+        in_specs=[scalars] + [hbm] * 6,
+        out_specs=(whole,) * 3,
         scratch_shapes=[
             vmem(prompts, span, width), vmem(width, HL * HD), vmem(width, 128), vmem(128, width), vmem(width, 128),
             vmem(*eq.shape), vmem(*sel.shape),
@@ -578,20 +597,21 @@
             vmem(prompts, HL, span, ROWS),
             vmem(prompts, HL, span, HD, kind=F32), vmem(prompts, HL, span, HD, kind=F32),
             vmem(prompts, HL, span, HD, kind=F32),
-            vmem(prompts, span, HL * HD), vmem(8, span, kind=F32), vmem(nx, 8, span, kind=F32),
+            vmem(8, span, kind=F32), vmem(nx, 8, span, kind=F32),
             vmem(prompts, 2, *block), vmem(prompts, *block), vmem(prompts, *block), vmem(ny, *block),
-            vmem(nz, zr, HD), vmem(nz, zr, HD), vmem(nz, zr, HD), vmem(nz, zr, HD), vmem(zr, HD), vmem(nz, zr, HD),
+            vmem(nz, zr, HD), vmem(2 * ROWS, HD, kind=F32), vmem(nz, zr, HD),
+            vmem(nz, zr, HD), vmem(nz, zr, HD), vmem(zr, HD), vmem(nz, zr, HD),
             vmem(ny, *block), vmem(prompts, *block), vmem(prompts, *block), vmem(prompts, *block),
             vmem(nx, part, HD), vmem(prompts, nx, part, HD), vmem(prompts, 2, ROWS - 128, HD),
-            dma((5,)), dma((prompts,)), dma((prompts,)), dma((prompts,)),
+            dma((11,)), dma((prompts, 4)), dma((prompts,)), dma((prompts,)),
             dma((ny,)), dma((ny,)), dma((nz,)), dma((nz,)), dma((nz,)), dma((nz,)), dma((nz,)), dma((nz,)),
             dma((ny,)), dma((ny,)), dma((prompts,)), dma((prompts,)),
             dma((nx,)), dma((nx,)), dma((ny,)), dma((ny,)), dma((ny,)), dma((ny,)),
             dma((ny,)), dma((ny,)), dma((ny,)), dma((ny,)),
-            dma((nx,)), dma((nx,)), dma((3 * prompts + 1,)),
+            dma((nx,)), dma((nx,)), dma((2 * prompts,)),
         ],
         compiler_params=pltpu.CompilerParams(
-            collective_id=0, has_side_effects=True, vmem_limit_bytes=60 * 1024 * 1024
+            collective_id=0, has_side_effects=True, vmem_limit_bytes=LIMIT1
         ),
         name="prefill",
     )(lengths, hidden_in, w_value, w_key, w_query, eq, sel)
@@ -605,16 +625,14 @@
             array(1, prompts, HL * nx, own),
             array(1, prompts, HL, FD + 1),
         ),
-        in_specs=[scalars] + [anyspace] * 4,
-        out_specs=(anyspace,) * 5,
+        in_specs=[scalars] + [whole] * 3 + [hbm],
+        out_specs=(hbm,) * 5,
         scratch_shapes=[
-            vmem(nc, prompts, nx, part, HD),
-            vmem(nc, prompts, 2, ROWS - 128, HD), vmem(own, ROWS), vmem(prompts, span, HL * HD),
-            vmem(prompts, HL * nx, own, HD, kind=F32), vmem(prompts, FD + 1, HL, HD, kind=F32),
+            vmem(own, ROWS), vmem(prompts + 1, HL * nx, own, HD, kind=F32), vmem(prompts, FD + 1, HL, HD, kind=F32),
             vmem(prompts, HL * nx, own, kind=F32), vmem(prompts, HL, FD + 1, kind=F32),
-            dma((2 * prompts + 2,)), dma((5 * prompts,)),
+            dma((1,)), dma((5 * prompts,)),
         ],
-        compiler_params=pltpu.CompilerParams(vmem_limit_bytes=60 * 1024 * 1024),
+        compiler_params=pltpu.CompilerParams(vmem_limit_bytes=LIMIT2),
         name="finish",
     )(owners, scaled, fx, low, sel)
     return mixed, quad, jnp.transpose(state_low, (0, 1, 3, 2, 4)), nquad, nlow

time: 49.4 us -> 48.5 us (0.982)
  Pallas kernels: 48.6 us -> 47.7 us
    pallas_call x1, Pallas kernels: 3.42 us -> 2.57 us  [body(): pl.pallas_call(functools.partial(finish, (nz, ny, nc, nx, prompts)), out_...]
where the time goes in v3:
time: 48.5 us; the launch traced here: 48.3 us
  Pallas kernels  47.7 us (98%)
  between operations  0.64 us (1%)
    pallas_call x1, Pallas kernels, body(): pl.pallas_call(functools.partial(kernel, (nz, ny, nc, nx, span, wide)), o...  45.1 us
    pallas_call x1, Pallas kernels, body(): pl.pallas_call(functools.partial(finish, (nz, ny, nc, nx, prompts)), out_...  2.57 us

profile of v3, /device:TPU:1, one launch (start us, length us, event | category | flops | bytes accessed | tf_op | source)
XLA Modules:
  0.0 48.3 jit_solution(3058855930697524065)
XLA Ops:
  0.6 45.1 %prefill.1 = (bf16[4,256,512]{2,1,0:T(8,128)(2,1)S(1)}, bf16[2,4,4,144,128]{4,3,2,1,0:T(8,128)(2,1)S(1)}, bf16[2,4,2,32,128]{4,3,2,1,0:T(8,128)(2,1)S(1)}) custom-call(s32[4]{0:T(128)} %len_ref.1, bf16[4,256,2048]{2,1,0:T(8,128)(2,1)} %hid_hbm.1, bf16[2048,512]{1,0:T(8,128)(2,1)} %wv_hbm.1, bf16[2048,256]{1,0:T(8,128)(2,1)} %wk_hbm.1, ...), custom_call_target="tpu_custom_call" | custom-call | tf_op jit(solution)/shard_map/prefill/pallas_call | solution.py:584
  45.8 2.6 %finish.1 = (bf16[4,256,512]{2,1,0:T(8,128)(2,1)}, f32[1,4,16,64,128]{4,3,2,1,0:T(8,128)}, f32[1,4,17,4,128]{4,3,2,1,0:T(4,128)}, f32[1,4,16,64]{3,2,1,0:T(8,128)}, f32[1,4,4,17]{3,2,1,0:T(4,128)}) custom-call(s32[4]{0:T(128)} %own_ref.1, bf16[4,256,512]{2,1,0:T(8,128)(2,1)S(1)} %get-tuple-element.13.mixed, ...), custom_call_target="tpu_custom_call" | custom-call | tf_op jit(solution)/shard_map/finish/pallas_call | solution.py:619

commit v4 on v3

--- a/solution.py
+++ b/solution.py
@@ -33,6 +33,15 @@
     if d == 8:
         return 8 * FD + min(i, j)
     return (FD - d) * FD + j
+
+
+def needed(x, nx):
+    own = FD // nx
+    return sorted({row_of(x * own + n // FD, n % FD) for n in range(own * FD)})
+
+
+def final_rows(nx):
+    return -(-(2 * len(needed(0, nx)) + 4) // 16) * 16
 
 
 @functools.cache
@@ -47,14 +56,26 @@
             eq[1, h, 65, LIN + i] = 1.0
         eq[0, h, 65, ONE] = eq[1, h, 65, ONE] = 1.0
     own = FD // nx
-    sel = np.zeros((nx, own * FD, ROWS), np.float32)
+    part = final_rows(nx)
+    sel = np.zeros((nx, part, 2 * ROWS), np.float32)
+    spread = np.zeros((nx, 2 * own * FD, part), np.float32)
+    pick = np.zeros((nx, own * FD, ROWS), np.float32)
     for x in range(nx):
-        for ii in range(own):
-            for j in range(FD):
-                sel[x, ii * FD + j, row_of(x * own + ii, j)] = 1.0
+        rows = needed(x, nx)
+        for i in range(2):
+            for n, r in enumerate(rows):
+                sel[x, i * len(rows) + n, i * ROWS + r] = 1.0
+            for r in range(2):
+                sel[x, 2 * len(rows) + 2 * i + r, i * ROWS + NORM + r] = 1.0
+            for n in range(own * FD):
+                r = row_of(x * own + n // FD, n % FD)
+                spread[x, i * own * FD + n, i * len(rows) + rows.index(r)] = 1.0
+                pick[x, n, r] = 1.0
     return (
         eq.reshape(2 * HL, 128, ROWS).astype(BF16),
-        sel.reshape(-1, ROWS).astype(BF16),
+        sel.reshape(-1, 2 * ROWS).astype(BF16),
+        spread.reshape(-1, part).astype(BF16),
+        pick.reshape(-1, ROWS).astype(BF16),
     )
 
 
@@ -149,6 +170,7 @@
     keyt[...] = jnp.zeros(keyt.shape, BF16)
     far_z = sorted(range(1, nz), key=lambda d: -min(d, nz - d))
     far_y = [d for d in (1, 3, 2) if d < ny]
+    far_x = [d for d in (2, 1, 3) if d < nx]
     ones = jnp.ones((8, span), BF16)
     sq[...] = jnp.zeros(sq.shape, F32)
 
@@ -235,19 +257,6 @@
     state(ny - 1)
     chip(y, True)
     ry[y] = csum[y]
-    for d in range(1, ny):
-        q = lax.rem(y + d, ny)
-        remote(csum.at[q], ry.at[q], sy.at[q], vy.at[q], at_y(q)).wait_recv()
-    total = ry[0].astype(F32)
-    for q in range(1, ny):
-        total = total + ry[q].astype(F32)
-    whole_total[...] = total.reshape(2 * ROWS, HD)
-    flat = whole_total[...]
-    for q in range(nz):
-        cut[q] = flat[q * zr : (q + 1) * zr].astype(BF16)
-    for d in far_z:
-        slice_to(lax.rem(z + d, nz)).start()
-    rz[z] = cut[z]
     for load in loads:
         load.wait()
 
@@ -272,7 +281,21 @@
         inside(p)
         return carry
 
-    lax.fori_loop(0, ny // 2, inside_step, 0)
+    lax.fori_loop(0, 1, inside_step, 0)
+    for d in range(1, ny):
+        q = lax.rem(y + d, ny)
+        remote(csum.at[q], ry.at[q], sy.at[q], vy.at[q], at_y(q)).wait_recv()
+    total = ry[0].astype(F32)
+    for q in range(1, ny):
+        total = total + ry[q].astype(F32)
+    whole_total[...] = total.reshape(2 * ROWS, HD)
+    flat = whole_total[...]
+    for q in range(nz):
+        cut[q] = flat[q * zr : (q + 1) * zr].astype(BF16)
+    for d in far_z:
+        slice_to(lax.rem(z + d, nz)).start()
+    rz[z] = cut[z]
+    lax.fori_loop(1, ny // 2, inside_step, 0)
 
     for d in range(1, nz):
         q = lax.rem(z + d, nz)
@@ -313,25 +336,23 @@
         prefix_to_y(lax.rem(y + d, ny)).start()
     rpy[y] = py[y]
 
-    own = sel.shape[0] // nx
+    part = sel.shape[0] // nx
     for d in range(1, nz):
         q = lax.rem(z + d, nz)
         remote(tt, rtt.at[q], sz3.at[q], vz3.at[q], at_z(q)).wait_recv()
-    whole = jnp.concatenate([rtt[q].astype(F32) for q in range(nz)], axis=0).reshape(2, ROWS, HD)
-    tails = jnp.concatenate([whole[0, ROWS - 8 :], whole[1, ROWS - 8 :]], axis=0).astype(BF16)
-    whole = whole.astype(BF16)
+    whole = jnp.concatenate([rtt[q] for q in range(nz)], axis=0) if zr % 16 == 0 else (
+        jnp.concatenate([rtt[q].astype(F32) for q in range(nz)], axis=0).astype(BF16)
+    )
+    picked = dot(sel[...], whole).astype(BF16)
+    for q in range(nx):
+        fxs[q] = picked[q * part : (q + 1) * part]
     for i in range(2):
-        picked = dot(sel[...], whole[i]).astype(BF16)
-        for q in range(nx):
-            fxs[q, i * own : (i + 1) * own] = picked[q * own : (q + 1) * own]
-        lowa[y, i] = whole[i, 128:]
-    for q in range(nx):
-        fxs[q, 2 * own :] = tails
+        lowa[y, i] = whole[i * ROWS + 128 : (i + 1) * ROWS]
 
     def final_to_x(q):
         return remote(fxs.at[q], fxa.at[y, x], sx.at[q], vx.at[x], at_x(q))
 
-    for d in range(1, nx):
+    for d in far_x:
         final_to_x(lax.rem(x + d, nx)).start()
     fxa[y, x] = fxs[x]
 
@@ -413,7 +434,7 @@
     def low_to_y(q):
         return remote(lowa.at[y], lowa.at[y], sy4.at[q], vy4.at[y], at_y(q))
 
-    for d in far_y:
+    for d in far_y[::-1]:
         q = lax.rem(y + d, ny)
         final_to_y(q).start()
         low_to_y(q).start()
@@ -432,7 +453,7 @@
     def square_to_x(q):
         return remote(sq, rsq.at[x], sx2.at[q], vx2.at[x], at_x(q))
 
-    for d in range(1, nx):
+    for d in far_x:
         square_to_x(lax.rem(x + d, nx)).start()
 
     rsq[x] = sq[...]
@@ -485,13 +506,14 @@
 
 
 def finish(
-    sizes, own_ref, mixed, fx, low, sel_hbm, mixed_hbm, quad_hbm, slow_hbm, nquad_hbm, nlow_hbm,
-    sel, quad, slow, nquad, nlow, isem, osem,
+    sizes, own_ref, mixed, fx, low, spread_hbm, pick_hbm, mixed_hbm, quad_hbm, slow_hbm, nquad_hbm, nlow_hbm,
+    spread, pick, quad, slow, nquad, nlow, isem, osem,
 ):
     nz, ny, nc, nx, prompts = sizes
     z, y, c, x = (lax.axis_index(a) for a in ("z", "y", "c", "x"))
     here = (z * ny + y) * nc + c
-    own = sel.shape[0]
+    own = pick.shape[0]
+    at_norm = 2 * len(needed(0, nx))
 
     def out_copies(p, at):
         return [
@@ -504,8 +526,14 @@
     def mixed_out(p):
         return pltpu.make_async_copy(mixed.at[p], mixed_hbm.at[p], osem.at[p])
 
-    sel_in = pltpu.make_async_copy(sel_hbm.at[pl.ds(pl.multiple_of(x * own, own), own)], sel, isem.at[0])
-    sel_in.start()
+    tables_in = [
+        pltpu.make_async_copy(
+            spread_hbm.at[pl.ds(pl.multiple_of(x * 2 * own, 2 * own), 2 * own)], spread, isem.at[0]
+        ),
+        pltpu.make_async_copy(pick_hbm.at[pl.ds(pl.multiple_of(x * own, own), own)], pick, isem.at[1]),
+    ]
+    for table in tables_in:
+        table.start()
     for p in range(prompts):
         mixed_out(p).start()
     quad[prompts] = jnp.zeros(quad.shape[1:], F32)
@@ -519,7 +547,8 @@
             for copy in out_copies(p, prompts):
                 copy.start()
 
-    sel_in.wait()
+    for table in tables_in:
+        table.wait()
     quad_scale = (2.0 * FD) ** (-0.5)
     low_scale = FD ** (-0.25)
     lin, one = LIN - 128, ONE - 128
@@ -530,14 +559,15 @@
             first, rest = [], []
             for g in range(nx):
                 for k in range(nc):
-                    block = fx[k, p, g].astype(F32)
+                    quads = dot(spread[...], fx[k, p, g])
+                    norms = fx[k, p, g].astype(F32)
                     for i in range(2):
-                        quad[p, g * HL + k * 2 + i] = block[i * own : (i + 1) * own] * quad_scale
-                        at = 2 * own + i * 8 + NORM - (ROWS - 8)
-                        first.append(block[at : at + 1])
-                        rest.append(block[at + 1 : at + 2, : ROWS - 128])
+                        quad[p, g * HL + k * 2 + i] = quads[i * own : (i + 1) * own] * quad_scale
+                        at = at_norm + 2 * i
+                        first.append(norms[at : at + 1])
+                        rest.append(norms[at + 1 : at + 2, : ROWS - 128])
             norms = jnp.concatenate([jnp.concatenate(first, axis=0), jnp.concatenate(rest, axis=0)], axis=1)
-            nquad[p] = dot(norms.astype(BF16), sel[...], 1, 1) * quad_scale
+            nquad[p] = dot(norms.astype(BF16), pick[...], 1, 1) * quad_scale
             for k in range(nc):
                 for i in range(2):
                     rows = low[k, p, i].astype(F32)
@@ -561,13 +591,13 @@
     nz, ny, nc, nx = (lax.axis_size(a) for a in ("z", "y", "c", "x"))
     prompts, span, width = hidden_in.shape
     own = FD // nx * FD
-    part = 2 * own + 16
+    part = final_rows(nx)
     zr = 2 * ROWS // nz
     wide = HD * HL * nx
-    eq, sel = (jnp.asarray(t) for t in tables(nx))
-    lengths, owners, hidden_in, w_value, w_key, w_query, eq, sel = (
+    eq, sel, spread, pick = (jnp.asarray(t) for t in tables(nx))
+    lengths, owners, hidden_in, w_value, w_key, w_query, eq, sel, spread, pick = (
         pltpu.with_memory_space_constraint(a, pltpu.HBM)
-        for a in (lengths, owners, hidden_in, w_value, w_key, w_query, eq, sel)
+        for a in (lengths, owners, hidden_in, w_value, w_key, w_query, eq, sel, spread, pick)
     )
     hbm = pl.BlockSpec(memory_space=pltpu.HBM)
     whole = pl.BlockSpec(memory_space=pltpu.VMEM)
@@ -625,16 +655,16 @@
             array(1, prompts, HL * nx, own),
             array(1, prompts, HL, FD + 1),
         ),
-        in_specs=[scalars] + [whole] * 3 + [hbm],
+        in_specs=[scalars] + [whole] * 3 + [hbm] * 2,
         out_specs=(hbm,) * 5,
         scratch_shapes=[
-            vmem(own, ROWS), vmem(prompts + 1, HL * nx, own, HD, kind=F32), vmem(prompts, FD + 1, HL, HD, kind=F32),
+            vmem(2 * own, part), vmem(own, ROWS), vmem(prompts + 1, HL * nx, own, HD, kind=F32), vmem(prompts, FD + 1, HL, HD, kind=F32),
             vmem(prompts, HL * nx, own, kind=F32), vmem(prompts, HL, FD + 1, kind=F32),
-            dma((1,)), dma((5 * prompts,)),
+            dma((2,)), dma((5 * prompts,)),
         ],
         compiler_params=pltpu.CompilerParams(vmem_limit_bytes=LIMIT2),
         name="finish",
-    )(owners, scaled, fx, low, sel)
+    )(owners, scaled, fx, low, spread, pick)
     return mixed, quad, jnp.transpose(state_low, (0, 1, 3, 2, 4)), nquad, nlow
 
 

time: 48.5 us -> 47.8 us (0.986)
  Pallas kernels: 47.7 us -> 47 us
    pallas_call x1, Pallas kernels: 45.1 us -> 44.4 us  [body(): pl.pallas_call(functools.partial(kernel, (nz, ny, nc, nx, span, wide)), o...]
where the time goes in v4:
time: 47.8 us; the launch traced here: 47.6 us
  Pallas kernels  47 us (98%)
  between operations  0.64 us (1%)
    pallas_call x1, Pallas kernels, body(): pl.pallas_call(functools.partial(kernel, (nz, ny, nc, nx, span, wide)), o...  44.4 us
    pallas_call x1, Pallas kernels, body(): pl.pallas_call(functools.partial(finish, (nz, ny, nc, nx, prompts)), out_...  2.58 us

profile of v4, /device:TPU:1, one launch (start us, length us, event | category | flops | bytes accessed | tf_op | source)
XLA Modules:
  0.0 47.6 jit_solution(524054092719545039)
XLA Ops:
  0.6 44.4 %prefill.1 = (bf16[4,256,512]{2,1,0:T(8,128)(2,1)S(1)}, bf16[2,4,4,128,128]{4,3,2,1,0:T(8,128)(2,1)S(1)}, bf16[2,4,2,32,128]{4,3,2,1,0:T(8,128)(2,1)S(1)}) custom-call(s32[4]{0:T(128)} %len_ref.1, bf16[4,256,2048]{2,1,0:T(8,128)(2,1)} %hid_hbm.1, bf16[2048,512]{1,0:T(8,128)(2,1)} %wv_hbm.1, bf16[2048,256]{1,0:T(8,128)(2,1)} %wk_hbm.1, ...), custom_call_target="tpu_custom_call" | custom-call | tf_op jit(solution)/shard_map/prefill/pallas_call | solution.py:614
  45.0 2.6 %finish.1 = (bf16[4,256,512]{2,1,0:T(8,128)(2,1)}, f32[1,4,16,64,128]{4,3,2,1,0:T(8,128)}, f32[1,4,17,4,128]{4,3,2,1,0:T(4,128)}, f32[1,4,16,64]{3,2,1,0:T(8,128)}, f32[1,4,4,17]{3,2,1,0:T(4,128)}) custom-call(s32[4]{0:T(128)} %own_ref.1, bf16[4,256,512]{2,1,0:T(8,128)(2,1)S(1)} %get-tuple-element.13.mixed, ...), custom_call_target="tpu_custom_call" | custom-call | tf_op jit(solution)/shard_map/finish/pallas_call | solution.py:649

commit v5 on v4

--- a/solution.py
+++ b/solution.py
@@ -86,9 +86,9 @@
 def kernel(
     sizes, len_ref, hid_hbm, wv_hbm, wk_hbm, wq_hbm, eq_hbm, sel_hbm, mixed, fx_all, low_all,
     hid, wv, wk, wkt, wq, eq, sel, val, keyt, kd, phi, nself, dself, att, sq, rsq,
-    loc, r0, csum, ry, cut, whole_total, rz, pz, rpz, tt, rtt, py, rpy, pc, rpc, fxs, fxa, lowa,
+    loc, r0, csum, ry, cut, whole_total, rz, pz, rpz, tt, rtt, py, rpy, pc, rpc, fxs,
     lsem, hsem, s0, v0, sy, vy, sz, vz, sz2, vz2, sz3, vz3, sy2, vy2, s02, v02,
-    sx, vx, sy3, vy3, sy4, vy4, s3, v3, s4, v4, sx2, vx2, osem,
+    sx, vx, sy3, vy3, sy4, vy4, s3, v3, s4, v4, sx2, vx2,
 ):
     nz, ny, nc, nx, span, width = sizes
     width_in = wk.shape[0]
@@ -347,14 +347,14 @@
     for q in range(nx):
         fxs[q] = picked[q * part : (q + 1) * part]
     for i in range(2):
-        lowa[y, i] = whole[i * ROWS + 128 : (i + 1) * ROWS]
+        low_all[c, y, i] = whole[i * ROWS + 128 : (i + 1) * ROWS]
 
     def final_to_x(q):
-        return remote(fxs.at[q], fxa.at[y, x], sx.at[q], vx.at[x], at_x(q))
+        return remote(fxs.at[q], fx_all.at[c, y, x], sx.at[q], vx.at[x], at_x(q))
 
     for d in far_x:
         final_to_x(lax.rem(x + d, nx)).start()
-    fxa[y, x] = fxs[x]
+    fx_all[c, y, x] = fxs[x]
 
 
     def attend(p, h, state):
@@ -395,20 +395,14 @@
         sq[pl.ds(p, 1)] = (dot(unit, high, 1, 1) + dot(unit, rest, 1, 1))[0:1]
 
     def final_to_core(p):
-        return remote(fxa.at[p], fx_all.at[c, p], s3.at[p], v3.at[p], core)
+        return remote(fx_all.at[c, p], fx_all.at[c, p], s3.at[p], v3.at[p], core)
 
     def low_to_core(p):
-        return remote(lowa.at[p], low_all.at[c, p], s4.at[p], v4.at[p], core)
-
-    def final_here(p):
-        return pltpu.make_async_copy(fxa.at[p], fx_all.at[c, p], osem.at[p])
-
-    def low_here(p):
-        return pltpu.make_async_copy(lowa.at[p], low_all.at[c, p], osem.at[ny + p])
+        return remote(low_all.at[c, p], low_all.at[c, p], s4.at[p], v4.at[p], core)
 
     def deliver(p):
-        for copy in (final_to_core(p), low_to_core(p), final_here(p), low_here(p)):
-            copy.start()
+        final_to_core(p).start()
+        low_to_core(p).start()
 
     def arrived(d):
         p = lax.rem(y + d, ny)
@@ -426,18 +420,19 @@
 
     for d in range(1, nx):
         q = lax.rem(x + d, nx)
-        remote(fxs.at[q], fxa.at[y, q], sx.at[q], vx.at[q], at_x(q)).wait_recv()
+        remote(fxs.at[q], fx_all.at[c, y, q], sx.at[q], vx.at[q], at_x(q)).wait_recv()
 
     def final_to_y(q):
-        return remote(fxa.at[y], fxa.at[y], sy3.at[q], vy3.at[y], at_y(q))
+        return remote(fx_all.at[c, y], fx_all.at[c, y], sy3.at[q], vy3.at[y], at_y(q))
 
     def low_to_y(q):
-        return remote(lowa.at[y], lowa.at[y], sy4.at[q], vy4.at[y], at_y(q))
+        return remote(low_all.at[c, y], low_all.at[c, y], sy4.at[q], vy4.at[y], at_y(q))
 
     for d in far_y[::-1]:
         q = lax.rem(y + d, ny)
         final_to_y(q).start()
-        low_to_y(q).start()
+    for d in far_y[::-1]:
+        low_to_y(lax.rem(y + d, ny)).start()
 
     deliver(y)
 
@@ -472,13 +467,16 @@
 
     for s in (3, 1, 2):
         q = lax.rem(y + s, ny)
-        remote(fxa.at[y], fxa.at[q], sy3.at[q], vy3.at[q], at_y(q)).wait_recv()
-        remote(lowa.at[y], lowa.at[q], sy4.at[q], vy4.at[q], at_y(q)).wait_recv()
-        deliver(q)
+        remote(fx_all.at[c, y], fx_all.at[c, q], sy3.at[q], vy3.at[q], at_y(q)).wait_recv()
+        final_to_core(q).start()
+    for s in (3, 1, 2):
+        q = lax.rem(y + s, ny)
+        remote(low_all.at[c, y], low_all.at[c, q], sy4.at[q], vy4.at[q], at_y(q)).wait_recv()
+        low_to_core(q).start()
 
     for p in range(ny):
-        remote(fxa.at[p], fx_all.at[other, p], s3.at[p], v3.at[p], core).wait_recv()
-        remote(lowa.at[p], low_all.at[other, p], s4.at[p], v4.at[p], core).wait_recv()
+        remote(fx_all.at[c, p], fx_all.at[other, p], s3.at[p], v3.at[p], core).wait_recv()
+        remote(low_all.at[c, p], low_all.at[other, p], s4.at[p], v4.at[p], core).wait_recv()
 
     for p in range(ny):
         to_core(p).wait_send()
@@ -501,8 +499,6 @@
     for p in range(ny):
         final_to_core(p).wait_send()
         low_to_core(p).wait_send()
-        final_here(p).wait()
-        low_here(p).wait()
 
 
 def finish(
@@ -632,13 +628,13 @@
             vmem(nz, zr, HD), vmem(2 * ROWS, HD, kind=F32), vmem(nz, zr, HD),
             vmem(nz, zr, HD), vmem(nz, zr, HD), vmem(zr, HD), vmem(nz, zr, HD),
             vmem(ny, *block), vmem(prompts, *block), vmem(prompts, *block), vmem(prompts, *block),
-            vmem(nx, part, HD), vmem(prompts, nx, part, HD), vmem(prompts, 2, ROWS - 128, HD),
+            vmem(nx, part, HD),
             dma((11,)), dma((prompts, 4)), dma((prompts,)), dma((prompts,)),
             dma((ny,)), dma((ny,)), dma((nz,)), dma((nz,)), dma((nz,)), dma((nz,)), dma((nz,)), dma((nz,)),
             dma((ny,)), dma((ny,)), dma((prompts,)), dma((prompts,)),
             dma((nx,)), dma((nx,)), dma((ny,)), dma((ny,)), dma((ny,)), dma((ny,)),
             dma((ny,)), dma((ny,)), dma((ny,)), dma((ny,)),
-            dma((nx,)), dma((nx,)), dma((2 * prompts,)),
+            dma((nx,)), dma((nx,)),
         ],
         compiler_params=pltpu.CompilerParams(
             collective_id=0, has_side_effects=True, vmem_limit_bytes=LIMIT1

time: 47.8 us -> 47.5 us (level)
  no operation moved by 1% of the time
where the time goes in v5:
time: 47.5 us; the launch traced here: 47.3 us
  Pallas kernels  46.7 us (98%)
  between operations  0.64 us (1%)
    pallas_call x1, Pallas kernels, body(): pl.pallas_call(functools.partial(kernel, (nz, ny, nc, nx, span, wide)), o...  44.1 us
    pallas_call x1, Pallas kernels, body(): pl.pallas_call(functools.partial(finish, (nz, ny, nc, nx, prompts)), out_...  2.58 us

profile of v5, /device:TPU:1, one launch (start us, length us, event | category | flops | bytes accessed | tf_op | source)
XLA Modules:
  0.0 47.3 jit_solution(6959527695298318537)
XLA Ops:
  0.6 44.1 %prefill.1 = (bf16[4,256,512]{2,1,0:T(8,128)(2,1)S(1)}, bf16[2,4,4,128,128]{4,3,2,1,0:T(8,128)(2,1)S(1)}, bf16[2,4,2,32,128]{4,3,2,1,0:T(8,128)(2,1)S(1)}) custom-call(s32[4]{0:T(128)} %len_ref.1, bf16[4,256,2048]{2,1,0:T(8,128)(2,1)} %hid_hbm.1, bf16[2048,512]{1,0:T(8,128)(2,1)} %wv_hbm.1, bf16[2048,256]{1,0:T(8,128)(2,1)} %wk_hbm.1, ...), custom_call_target="tpu_custom_call" | custom-call | tf_op jit(solution)/shard_map/prefill/pallas_call | solution.py:610
  44.8 2.6 %finish.1 = (bf16[4,256,512]{2,1,0:T(8,128)(2,1)}, f32[1,4,16,64,128]{4,3,2,1,0:T(8,128)}, f32[1,4,17,4,128]{4,3,2,1,0:T(4,128)}, f32[1,4,16,64]{3,2,1,0:T(8,128)}, f32[1,4,4,17]{3,2,1,0:T(4,128)}) custom-call(s32[4]{0:T(128)} %own_ref.1, bf16[4,256,512]{2,1,0:T(8,128)(2,1)S(1)} %get-tuple-element.13.mixed, ...), custom_call_target="tpu_custom_call" | custom-call | tf_op jit(solution)/shard_map/finish/pallas_call | solution.py:645
